TPU v7x, 32 devices: a whole 2x2x4 slice. The times are simulated.
32 devices in a mesh: grp: 2 (over x), leaf: 16 (over z, y, core).
Axes of the slice: x: 2, y: 2, z: 4, core: 2. Of those that a mesh axis runs over, the one named last changes fastest.
Arguments:
- points: float32 [8, 32768], P(None, ('grp', 'leaf')), may hold values from -6 to 6
- rhs: float32 [16, 32768], P(None, ('grp', 'leaf')), may hold values from -6 to 6
- basis: float32 [32768, 128], P(('grp', 'leaf')), may hold values from -0.1875 to 0.1875
- transfer: float32 [32, 128, 128], P(('grp', 'leaf')), may hold values from -0.5 to 0.5
- noise: float32 [32768], P(('grp', 'leaf')), may hold values from 0.5 to 2
- inv_scale: float32 [8], replicated, may hold values from 0.15 to 0.6
- links: int32 [32, 2], P(('grp', 'leaf')), may hold values from 0 to 1, as said below
- leaf_skel: int32 [32, 128], P(('grp', 'leaf')), may hold values from 0 to 1023, as said below
- group_skel: int32 [2, 128], P('grp'), may hold values from 0 to 2047, as said below
Outputs:
- solution: float32 [16, 32768], P(None, ('grp', 'leaf'))
- residual: float32 [16, 32768], P(None, ('grp', 'leaf'))
Inputs may be any that keep to these rules, and one draw needn't show every extreme that they name: `links`: column 1 of box l equals column 0 of box l + 1; column 0 is 0 for the first box of each group of 16 and column 1 for the last. `leaf_skel`: the 128 indices of a box are distinct. `group_skel`: the 128 indices of a group are distinct.
All inputs are finite; a program needn't handle non-finite values.
Results may differ from a plain program's by a relative error of at most 0.0003.
Values sent between devices are 32-bit elements; how exact they have to be, the bound alone decides.
No kernel may reach another device: no remote copies, remote signals or barrier semaphores. Data moves between devices by JAX's collectives and lax.ppermute only.
A program may use at most 128 MiB of HBM per device.

v0:
```python
import functools
import math

import jax
import jax.numpy as jnp
from jax import lax
from jax.experimental import pallas as pl
from jax.experimental.pallas import tpu as pltpu
from jax.sharding import PartitionSpec as P


F32 = jnp.float32
BF16 = jnp.bfloat16
LOG2E = math.log2(math.e)
UNIT = math.sqrt(5.0)
THIRD = 1.0 / 3.0
MIB = 1 << 20
SHIFT = 3.0


def raw(first, second):
    return lax.dot_general(
        first, second, (((1,), (0,)), ((), ())), preferred_element_type=F32
    )


def raw_t(first, second):
    return lax.dot_general(
        first, second, (((1,), (1,)), ((), ())), preferred_element_type=F32
    )


def split3(value):
    high = value.astype(BF16).astype(F32)
    rest = value - high
    middle = rest.astype(BF16).astype(F32)
    return high, middle, (rest - middle).astype(BF16).astype(F32)


def split2(value):
    high = value.astype(BF16)
    return high, (value - high.astype(F32)).astype(BF16)


def triple(value):
    return jnp.concatenate(split3(value), axis=0).astype(BF16)


def fold(value):
    rows = value.shape[0] // 3
    return value[0:rows] + value[rows : 2 * rows] + value[2 * rows :]


def pair(value):
    return jnp.concatenate(split2(value), axis=1)


def times(first, second):
    half = second.shape[1] // 2
    both = fold(raw(triple(first), second))
    return both[:, :half] + both[:, half:]


def times_t(first, second):
    parts = triple(first)
    return fold(raw_t(jnp.concatenate([parts, parts], axis=1), second))


def times_parts_t(first, high, low):
    parts = triple(first)
    return fold(raw_t(parts, high) + raw_t(parts, low))


def norm_rows(scaled):
    high, middle, low = split3(jnp.sum(scaled * scaled, axis=0, keepdims=True))
    one = jnp.ones_like(high)
    zero = jnp.zeros((2,) + high.shape[1:], F32)
    return high, middle, low, one, zero


def stack_left(scaled):
    high, middle, low = split3(scaled)
    n_high, n_middle, n_low, one, zero = norm_rows(scaled)
    norms = jnp.concatenate([n_high, n_middle, n_low, one, one, one, zero], axis=0)
    rows = [high, high, middle, middle, high, low, norms]
    used = 6 * scaled.shape[0] + 8
    rows.append(jnp.zeros((128 - used, scaled.shape[1]), F32))
    return jnp.concatenate(rows, axis=0).T.astype(BF16)


def stack_right(scaled):
    high, middle, low = split3(-2.0 * scaled)
    n_high, n_middle, n_low, one, zero = norm_rows(scaled)
    norms = jnp.concatenate([one, one, one, n_high, n_middle, n_low, zero], axis=0)
    rows = [high, middle, high, middle, low, high, norms]
    used = 6 * scaled.shape[0] + 8
    rows.append(jnp.zeros((128 - used, scaled.shape[1]), F32))
    return jnp.concatenate(rows, axis=0).astype(BF16)


def matern3(square):
    square = jnp.maximum(square, 1e-30)
    root = square * lax.rsqrt(square)
    base = root + 1.5
    return (base * base + 0.75) * jnp.exp2(root * (-LOG2E))


def to_row(column):
    shape = (column.shape[0], 128)
    mask = lax.broadcasted_iota(jnp.int32, shape, 0) == lax.broadcasted_iota(jnp.int32, shape, 1)
    return jnp.sum(jnp.where(mask, column, 0.0), axis=0, keepdims=True)


def to_column(row, rows, start=0):
    shape = (rows, 128)
    lane = lax.broadcasted_iota(jnp.int32, shape, 1)
    mask = lane == lax.broadcasted_iota(jnp.int32, shape, 0) + start
    return jnp.sum(jnp.where(mask, row, 0.0), axis=1, keepdims=True)


def row_sum(value):
    return jnp.sum(value, axis=1, keepdims=True)


def each(count, body, init):
    if count <= 16:
        for index in range(count):
            init = body(index, init)
        return init
    return lax.fori_loop(0, count, body, init)


def fill(ref, block):
    def put(index, carry):
        ref[index] = block
        return carry

    each(ref.shape[0], put, 0)


def call(kernel, outs, ins, space=pltpu.VMEM, scratch=(), limit=8, flops=1_000_000):
    return pl.pallas_call(
        kernel,
        out_shape=[jax.ShapeDtypeStruct(s, d) for s, d in outs],
        in_specs=[pl.BlockSpec(memory_space=space) for _ in ins],
        out_specs=[pl.BlockSpec(memory_space=pltpu.VMEM) for _ in outs],
        scratch_shapes=list(scratch),
        compiler_params=pltpu.CompilerParams(vmem_limit_bytes=limit * MIB),
        cost_estimate=pl.CostEstimate(flops=flops, bytes_accessed=1 << 20, transcendentals=0),
    )(*ins)


def prepare_kernel(
    points_hbm, rhs_hbm, basis_hbm, lift_hbm, noise_hbm, scale_hbm, links_hbm, skel_hbm,
    beside_ref, send_ref, weight_ref,
    points_ref, rhs_ref, basis_ref, lift_ref, noise_ref, scale_ref, links_ref, skel_ref, sems,
):
    sources = (points_hbm, scale_hbm, links_hbm, rhs_hbm, basis_hbm, skel_hbm, lift_hbm, noise_hbm)
    targets = (points_ref, scale_ref, links_ref, rhs_ref, basis_ref, skel_ref, lift_ref, noise_ref)
    copies = [
        pltpu.make_async_copy(source, target, sems.at[index])
        for index, (source, target) in enumerate(zip(sources, targets))
    ]
    for copy in copies:
        copy.start()
    for copy in copies:
        copy.wait()
    dim, width = points_ref.shape
    rhs_rows = rhs_ref.shape[0]
    _, rows, skel = send_ref.shape
    sub = lax.broadcasted_iota(jnp.int32, (dim, 1), 0)
    scale = jnp.zeros((dim, 1), F32)
    for d in range(dim):
        scale = jnp.where(sub == d, scale_ref[d], scale)
    scaled = points_ref[...] * scale * UNIT
    rhs = rhs_ref[...]
    beside_ref[0:dim, :] = scaled
    beside_ref[dim:, :] = rhs
    lower, upper = links_ref[0, 0].astype(F32), links_ref[0, 1].astype(F32)
    odd = lax.rem(lax.axis_index("leaf"), 2).astype(F32)
    own = 1.0 + lower + upper
    first = odd * lower + (1.0 - odd) * upper
    second = odd * upper + (1.0 - odd) * lower
    sub = lax.broadcasted_iota(jnp.int32, weight_ref.shape, 0)
    weight = jnp.where(sub == 0, own, jnp.where(sub == 1, first, second))
    weight_ref[...] = weight * THIRD
    pick = lax.broadcasted_iota(jnp.int32, (width, skel), 0) == skel_ref[...]
    chosen = fold(raw(triple(scaled), jnp.where(pick, 1.0, 0.0).astype(BF16)))
    coeff = times(rhs, pair(basis_ref[...]))
    lifted = times(coeff, pair(lift_ref[0]))
    parts = [chosen, coeff, lifted]
    if rows > dim + 2 * rhs_rows:
        parts.append(jnp.zeros((rows - dim - 2 * rhs_rows, skel), F32))
    fill(send_ref, jnp.concatenate(parts, axis=0))


def near_kernel(weight_ref, own_ref, other_ref, vec_ref, out_ref, *, kind):
    rhs_rows, width = out_ref.shape
    dim = own_ref.shape[0] - rhs_rows
    start = vec_ref.shape[0] - rhs_rows
    block = min(256, width)
    left = stack_left(other_ref[0:dim, :])
    right = stack_right(own_ref[0:dim, :])
    vec = triple(vec_ref[start:, :])
    weight = weight_ref[kind : kind + 1, 0:1]
    for c in range(width // block):
        cols = slice(c * block, (c + 1) * block)
        total = jnp.zeros((3 * rhs_rows, block), F32)
        for i in range(width // block):
            rows = slice(i * block, (i + 1) * block)
            high, low = split2(matern3(raw(left[rows], right[:, cols])))
            total = total + raw(vec[:, rows], high) + raw(vec[:, rows], low)
        out_ref[:, cols] = fold(total) * weight


def group_kernel(got_ref, pick_ref, out_ref, *, dim, rhs_rows):
    boxes, rows, skel = got_ref.shape
    start = dim + rhs_rows

    def body(index, carry):
        chosen, summed = carry
        block = got_ref[index]
        pick = lax.broadcasted_iota(jnp.int32, (skel, skel), 0) + index * skel == pick_ref[...]
        pick = jnp.where(pick, 1.0, 0.0).astype(BF16)
        return chosen + raw(triple(block[0:dim]), pick), summed + block[start:]

    zero = (jnp.zeros((3 * dim, skel), F32), jnp.zeros((rows - start, skel), F32))
    chosen, summed = each(boxes, body, zero)
    out_ref[0:dim, :] = fold(chosen)
    out_ref[dim:, :] = summed


def box_chunks(boxes):
    step = min(boxes, 16)
    while boxes % step:
        step -= 1
    return step, boxes // step


def far_kernel(got_ref, mine_ref, high_ref, low_ref, out_ref, *, dim):
    rhs_rows, skel = out_ref.shape
    step, count = box_chunks(got_ref.shape[0])
    left = stack_left(mine_ref[0, 0:dim, :])

    def body(index, total):
        blocks = [got_ref[index * step + j] for j in range(step)]
        right = stack_right(jnp.concatenate([block[0:dim] for block in blocks], axis=1))
        coeff = jnp.concatenate([block[dim : dim + rhs_rows] for block in blocks], axis=1)
        high, low = split2(matern3(raw(left, right)))
        high_ref[index] = high
        low_ref[index] = low
        return total + times_parts_t(coeff, high, low)

    out_ref[...] = each(count, body, jnp.zeros((rhs_rows, skel), F32)) * THIRD


def far_again_kernel(got_ref, high_ref, low_ref, out_ref):
    rhs_rows, skel = out_ref.shape
    step, count = box_chunks(got_ref.shape[0])

    def body(index, total):
        blocks = [got_ref[index * step + j, 0:rhs_rows, :] for j in range(step)]
        coeff = jnp.concatenate(blocks, axis=1)
        return total + times_parts_t(coeff, high_ref[index], low_ref[index])

    out_ref[...] = each(count, body, jnp.zeros((rhs_rows, skel), F32)) * THIRD


def sum_kernel(got_ref, out_ref):
    start = got_ref.shape[1] - out_ref.shape[0]

    def body(index, total):
        return total + got_ref[index, start:, :]

    out_ref[...] = each(got_ref.shape[0], body, jnp.zeros(out_ref.shape, F32))


def first_image_kernel(*refs, dim, groups):
    group_refs = refs[0:groups]
    (far_ref, near_ref, near_a_ref, near_b_ref, rhs_ref, noise_ref, lift_ref, basis_ref,
     shift_ref, send_ref, high_ref, low_ref) = refs[groups:]
    rhs_rows = rhs_ref.shape[0]
    _, rows, skel = send_ref.shape
    left = stack_left(group_refs[0][0:dim, :])
    right = stack_right(jnp.concatenate([ref[0:dim, :] for ref in group_refs], axis=1))
    high, low = split2(matern3(raw(left, right)))
    high_ref[...] = high
    low_ref[...] = low
    start = dim + rhs_rows
    coeff = jnp.concatenate([ref[dim:start, :] for ref in group_refs], axis=1)
    top = times_parts_t(coeff, high, low) * THIRD
    rhs = rhs_ref[...]
    basis = pair(basis_ref[...])
    lift = pair(lift_ref[0])
    row = far_ref[...] + times_t(top, lift)
    near = near_ref[...] + near_a_ref[...] + near_b_ref[...]
    shift = (noise_ref[...] - SHIFT) * rhs + near + times_t(row, basis)
    shift_ref[...] = shift
    coeff = times(shift, basis)
    lifted = times(coeff, lift)
    total = to_row(row_sum(rhs * rhs))
    along = to_row(row_sum(rhs * shift))
    rest = jnp.zeros((rows - 2 * rhs_rows - 2, skel), F32)
    fill(send_ref, jnp.concatenate([coeff, lifted, total, along, rest], axis=0))


def second_image_kernel(*refs, groups):
    group_refs = refs[0:groups]
    (far_ref, near_ref, near_a_ref, near_b_ref, rhs_ref, shift_ref, noise_ref,
     lift_ref, basis_ref, high_ref, low_ref,
     residual_ref, image_ref, alpha_ref, send_ref) = refs[groups:]
    rhs_rows = rhs_ref.shape[0]
    skel = lift_ref.shape[2]
    coeff = jnp.concatenate([ref[0:rhs_rows, :] for ref in group_refs], axis=1)
    top = times_parts_t(coeff, high_ref[...], low_ref[...]) * THIRD
    sums = sum(ref[rhs_rows : rhs_rows + 8, :] for ref in group_refs)
    total = to_column(sums[0:1], rhs_rows)
    along = to_column(sums[1:2], rhs_rows)
    curve = along + SHIFT * total
    alpha = total / curve
    keep = along / curve
    shift = shift_ref[...]
    rhs = rhs_ref[...]
    row = far_ref[...] + times_t(top, pair(lift_ref[0]))
    near = near_ref[...] + near_a_ref[...] + near_b_ref[...]
    second = noise_ref[...] * shift + near + times_t(row, pair(basis_ref[...]))
    residual = keep * rhs - alpha * shift
    image = keep * (shift + SHIFT * rhs) - alpha * second
    residual_ref[...] = residual
    image_ref[...] = image
    lane = lax.broadcasted_iota(jnp.int32, (rhs_rows, skel), 1)
    index = lax.broadcasted_iota(jnp.int32, (rhs_rows, skel), 0)
    alpha_ref[...] = jnp.where(lane == 0, alpha, total)
    both = jnp.where(lane == index, row_sum(residual * residual), 0.0)
    both = both + jnp.where(lane == index + rhs_rows, row_sum(residual * image), 0.0)
    fill(send_ref, jnp.sum(both, axis=0, keepdims=True))


def finish_kernel(
    got_ref, alpha_ref, rhs_ref, shift_ref, residual_ref, image_ref, solution_ref, out_ref
):
    rhs_rows = rhs_ref.shape[0]
    sums = jnp.sum(got_ref[...], axis=0)
    norm_next = to_column(sums, rhs_rows)
    curve = to_column(sums, rhs_rows, rhs_rows)
    alpha = alpha_ref[:, 0:1]
    norm_now = alpha_ref[:, 1:2]
    ratio = norm_next / norm_now
    step = norm_next / (curve - ratio * norm_next / alpha)
    rhs = rhs_ref[...]
    residual = residual_ref[...]
    image = shift_ref[...] + SHIFT * rhs
    solution_ref[...] = alpha * rhs + step * (residual + ratio * rhs)
    out_ref[...] = residual - step * (image_ref[...] + ratio * image)


def spread(value, axis):
    return lax.all_to_all(value, axis, 0, 0, tiled=True)


def pass_on(value, pairs):
    return lax.ppermute(value, "leaf", pairs)


def local(points, rhs, basis, transfer, noise, inv_scale, links, leaf_skel, group_skel):
    dim, width = points.shape
    rhs_rows = rhs.shape[0]
    skel = basis.shape[1]
    boxes = lax.axis_size("leaf")
    groups = lax.axis_size("grp")
    noise = noise[None, :]
    pairs_a = [(i, i ^ 1) for i in range(boxes) if (i ^ 1) < boxes]
    pairs_b = [(i, ((i + 1) ^ 1) - 1) for i in range(boxes) if 0 <= ((i + 1) ^ 1) - 1 < boxes]
    wide = (rhs_rows, width)
    small = (rhs_rows, skel)
    step, count = box_chunks(boxes)

    rows = -(-(dim + 2 * rhs_rows) // 8) * 8
    inputs = [points, rhs, basis, transfer, noise, inv_scale, links, leaf_skel]
    scratch = [pltpu.VMEM(value.shape, value.dtype) for value in inputs]
    for index in (5, 6):
        scratch[index] = pltpu.SMEM(inputs[index].shape, inputs[index].dtype)
    beside, send, weight = call(
        prepare_kernel,
        [((dim + rhs_rows, width), F32), ((boxes, rows, skel), F32), ((8, skel), F32)],
        inputs, space=pltpu.HBM, scratch=scratch + [pltpu.SemaphoreType.DMA((8,))],
        limit=60,
    )
    got = spread(send, "leaf")
    beside_a = pass_on(beside, pairs_a)
    beside_b = pass_on(beside, pairs_b)

    def near_part(other, vec, kind):
        return call(
            functools.partial(near_kernel, kind=kind), [(wide, F32)],
            [weight, beside, other, vec], limit=16, flops=4 * 10**9,
        )[0]

    near = near_part(beside, beside, 0)
    near_a = near_part(beside_a, beside_a, 1)
    near_b = near_part(beside_b, beside_b, 2)

    def exchange(value):
        return [value] + [
            lax.ppermute(value, "grp", [(i, (i + s) % groups) for i in range(groups)])
            for s in range(1, groups)
        ]

    (mine,) = call(
        functools.partial(group_kernel, dim=dim, rhs_rows=rhs_rows),
        [((rows - rhs_rows, skel), F32)], [got, group_skel],
    )
    parts = exchange(mine)
    far_shape = ((count, skel, step * skel), BF16)
    far_high, far_low, far = call(
        functools.partial(far_kernel, dim=dim), [far_shape, far_shape, (small, F32)], [got, send],
        limit=16, flops=10**9,
    )
    rows_next = -(-(2 * rhs_rows + 2) // 8) * 8
    top_shape = ((skel, groups * skel), BF16)
    shift, send, top_high, top_low = call(
        functools.partial(first_image_kernel, dim=dim, groups=groups),
        [(wide, F32), ((boxes, rows_next, skel), F32), top_shape, top_shape],
        [*parts, far, near, near_a, near_b, rhs, noise, transfer, basis],
    )
    got = spread(send, "leaf")
    shift_a = pass_on(shift, pairs_a)
    shift_b = pass_on(shift, pairs_b)
    near = near_part(beside, shift, 0)
    near_a = near_part(beside_a, shift_a, 1)
    near_b = near_part(beside_b, shift_b, 2)
    (mine,) = call(sum_kernel, [((rows_next - rhs_rows, skel), F32)], [got])
    parts = exchange(mine)
    (far,) = call(far_again_kernel, [(small, F32)], [got, far_high, far_low], flops=10**8)
    residual, image, alpha, send = call(
        functools.partial(second_image_kernel, groups=groups),
        [(wide, F32), (wide, F32), (small, F32), ((boxes * groups, 1, skel), F32)],
        [*parts, far, near, near_a, near_b, rhs, shift, noise, transfer, basis,
         top_high, top_low],
    )
    got = spread(send, ("grp", "leaf"))
    return tuple(
        call(
            finish_kernel, [(wide, F32), (wide, F32)],
            [got, alpha, rhs, shift, residual, image],
        )
    )


def solution(mesh):
    return jax.shard_map(
        local,
        mesh=mesh,
        in_specs=(
            P(None, ("grp", "leaf")),
            P(None, ("grp", "leaf")),
            P(("grp", "leaf"), None),
            P(("grp", "leaf"), None, None),
            P(("grp", "leaf")),
            P(),
            P(("grp", "leaf"), None),
            P(("grp", "leaf"), None),
            P("grp", None),
        ),
        out_specs=(P(None, ("grp", "leaf")), P(None, ("grp", "leaf"))),
        check_vma=False,
    )
```

profile of v0, /device:TPU:0, one launch (start us, length us, event | category | flops | bytes accessed | tf_op | source)
XLA Modules:
  0.0 62.9 jit_solution(9898378323521314612)
XLA Ops:
  0.6 2.3 %shard_map.104 = (f32[24,1024]{1,0:T(8,128)}, f32[16,40,128]{2,1,0:T(8,128)}, f32[8,128]{1,0:T(8,128)}) custom-call(f32[8,1024]{1,0:T(8,128)} %points_hbm.1, f32[16,1024]{1,0:T(8,128)} %rhs_ref.1, f32[1024,128]{1,0:T(8,128)} %refs_10_.1, f32[1,128,128]{2,1,0:T(8,128)} %refs_9_.3, f32[1,1024]{1,0:T(1,128)} %bitcast.1, f32[8]{0:T(128)} %scale_hbm.1, ...), custom_call_target="tpu_custom_call" | custom-call | flops 1000000 | bytes 1048576 | tf_op jit(solution)/shard_map/pallas_call | solution.py:142
  2.9 0.6 collective-permute-start.1
  3.5 0.7 %collective-permute-start.2 = (f32[24,1024]{1,0:T(8,128)}, f32[24,1024]{1,0:T(8,128)S(1)}, u32[]{:S(2)}, u32[]{:S(2)}) collective-permute-start(f32[24,1024]{1,0:T(8,128)} %get-tuple-element.19.own_ref.other_ref.vec_ref), channel_id=1, source_target_pairs={{1,2},{2,1},{3,4},{4,3},{5,6},{6,5},{7,8},{8,7},{9,10},{10,9},{11,... | collective-permute-start | bytes 294920 | tf_op jit(solution)/shard_map/ppermute | solution.py:362
  4.2 0.0 copy-start.6
  4.2 0.0 copy-start.7
  4.2 8.9 %all-to-all-start = ((f32[16,40,128]{2,1,0:T(8,128)}), f32[16,40,128]{2,1,0:T(8,128)S(1)}, u32[]{:S(2)}, u32[]{:S(2)}) async-start(f32[16,40,128]{2,1,0:T(8,128)} %get-tuple-element.16.mine_ref), calls=%async_computation | async-start | bytes 655360 | tf_op jit(solution)/shard_map/all_to_all | solution.py:358
  13.1 0.0 copy-done.6
  13.1 0.0 copy-done.7
  13.1 2.3 %shard_map.107.refs_3_ = f32[16,1024]{1,0:T(8,128)S(1)} custom-call(f32[8,128]{1,0:T(8,128)S(1)} %copy-done.7, f32[24,1024]{1,0:T(8,128)S(1)} %copy-done.6, f32[24,1024]{1,0:T(8,128)S(1)} %copy-done.6, f32[24,1024]{1,0:T(8,128)S(1)} %copy-done.6), custom_call_target="tpu_custom_call" | custom-call | flops 4000000000 | bytes 1048576 | tf_op jit(solution)/shard_map/pallas_call | solution.py:142
  15.4 0.0 collective-permute-done.1.other_ref.vec_ref
  15.4 2.3 %shard_map.108.refs_4_ = f32[16,1024]{1,0:T(8,128)S(1)} custom-call(f32[8,128]{1,0:T(8,128)S(1)} %copy-done.7, f32[24,1024]{1,0:T(8,128)S(1)} %copy-done.6, f32[24,1024]{1,0:T(8,128)S(1)} %collective-permute-done.1.other_ref.vec_ref, f32[24,1024]{1,0:T(8,128)S(1)} %collective-permute-done.1.other_ref.vec_ref), custom_call_target="tpu_custom_call" | custom-call | flops 4000000000 | bytes 1048576 | tf_op jit(solution)/shard_map/pallas_call | solution.py:142
  17.7 0.0 copy-start.5
  17.7 0.0 collective-permute-done.2.other_ref.vec_ref
  17.7 2.3 %shard_map.109.refs_5_ = f32[16,1024]{1,0:T(8,128)S(1)} custom-call(f32[8,128]{1,0:T(8,128)S(1)} %copy-done.7, f32[24,1024]{1,0:T(8,128)S(1)} %copy-done.6, f32[24,1024]{1,0:T(8,128)S(1)} %collective-permute-done.2.other_ref.vec_ref, f32[24,1024]{1,0:T(8,128)S(1)} %collective-permute-done.2.other_ref.vec_ref), custom_call_target="tpu_custom_call" | custom-call | flops 4000000000 | bytes 1048576 | tf_op jit(solution)/shard_map/pallas_call | solution.py:142
  20.0 0.0 copy-start.3
  20.0 4.2 %all-to-all-done.got_ref = f32[16,40,128]{2,1,0:T(8,128)S(1)} async-done(((f32[16,40,128]{2,1,0:T(8,128)}), f32[16,40,128]{2,1,0:T(8,128)S(1)}, u32[]{:S(2)}, u32[]{:S(2)}) %all-to-all-start) | async-done | bytes 327712 | tf_op jit(solution)/shard_map/all_to_all | solution.py:358
  24.2 0.0 copy-done.5
  24.2 0.2 shard_map.105.refs_0_
  24.4 0.0 copy-start
  24.5 0.0 copy-start.1
  24.5 0.0 copy-start.2
  24.5 1.6 %collective-permute-start = (f32[24,128]{1,0:T(8,128)S(1)}, f32[24,128]{1,0:T(8,128)S(1)}, u32[]{:S(2)}, u32[]{:S(2)}) collective-permute-start(f32[24,128]{1,0:T(8,128)S(1)} %shard_map.105.refs_0_), channel_id=1, source_target_pairs={{0,16},{16,0},{1,17},{17,1},{2,18},{18,2},{3,19},{19,3},{4,20},{20... | collective-permute-start | bytes 36872 | tf_op jit(solution)/shard_map/ppermute | solution.py:405
  26.0 0.0 copy-done.3
  26.0 0.0 copy-start.4
  26.0 1.1 %shard_map.106 = (bf16[1,128,2048]{2,1,0:T(8,128)(2,1)S(1)}, bf16[1,128,2048]{2,1,0:T(8,128)(2,1)S(1)}, f32[16,128]{1,0:T(8,128)S(1)}) custom-call(f32[16,40,128]{2,1,0:T(8,128)S(1)} %all-to-all-done.got_ref, f32[16,40,128]{2,1,0:T(8,128)S(1)} %copy-done.3), custom_call_target="tpu_custom_call" | custom-call | flops 1000000000 | bytes 1048576 | tf_op jit(solution)/shard_map/pallas_call | solution.py:142
  27.2 1.1 %collective-permute-done.refs_1_ = f32[24,128]{1,0:T(8,128)S(1)} collective-permute-done((f32[24,128]{1,0:T(8,128)S(1)}, f32[24,128]{1,0:T(8,128)S(1)}, u32[]{:S(2)}, u32[]{:S(2)}) %collective-permute-start) | collective-permute-done | bytes 12320 | tf_op jit(solution)/shard_map/ppermute | solution.py:405
  28.2 0.0 copy-done
  28.2 0.0 copy-done.1
  28.2 0.0 copy-done.2
  28.3 0.0 copy-done.4
  28.3 1.8 %shard_map.110 = (f32[16,1024]{1,0:T(8,128)S(1)}, f32[16,40,128]{2,1,0:T(8,128)}, bf16[128,256]{1,0:T(8,128)(2,1)S(1)}, bf16[128,256]{1,0:T(8,128)(2,1)S(1)}) custom-call(f32[24,128]{1,0:T(8,128)S(1)} %shard_map.105.refs_0_, f32[24,128]{1,0:T(8,128)S(1)} %collective-permute-done.refs_1_, f32[16,128]{1,0:T(8,128)S(1)} %get-tuple-element.17.refs_2_, ...), custom_call_target="tpu_custom_call" | custom-call | flops 1000000 | bytes 1048576 | tf_op jit(solution)/shard_map/pallas_call | solution.py:142
  30.1 0.7 %collective-permute-start.5 = (f32[16,1024]{1,0:T(8,128)S(1)}, f32[16,1024]{1,0:T(8,128)S(1)}, u32[]{:S(2)}, u32[]{:S(2)}) collective-permute-start(f32[16,1024]{1,0:T(8,128)S(1)} %get-tuple-element.23.vec_ref.refs_7_.shift_ref), channel_id=1, source_target_pairs={{1,2},{2,1},{3,4},{4,3},{5,6},{6,5},{7,8},{8,7},{9,10},{10,9},{11,... | collective-permute-start | bytes 196616 | tf_op jit(solution)/shard_map/ppermute | solution.py:362
  30.7 1.0 %collective-permute-start.4 = (f32[16,1024]{1,0:T(8,128)S(1)}, f32[16,1024]{1,0:T(8,128)S(1)}, u32[]{:S(2)}, u32[]{:S(2)}) collective-permute-start(f32[16,1024]{1,0:T(8,128)S(1)} %get-tuple-element.23.vec_ref.refs_7_.shift_ref), channel_id=1, source_target_pairs={{0,1},{1,0},{2,3},{3,2},{4,5},{5,4},{6,7},{7,6},{8,9},{9,8},{10,11... | collective-permute-start | bytes 196616 | tf_op jit(solution)/shard_map/ppermute | solution.py:362
  31.8 4.6 %all-to-all-start.1 = ((f32[16,40,128]{2,1,0:T(8,128)}), f32[16,40,128]{2,1,0:T(8,128)S(1)}, u32[]{:S(2)}, u32[]{:S(2)}) async-start(f32[16,40,128]{2,1,0:T(8,128)} %get-tuple-element.20), calls=%async_computation.1 | async-start | bytes 655360 | tf_op jit(solution)/shard_map/all_to_all | solution.py:358
  36.4 2.3 %shard_map.113.refs_3_ = f32[16,1024]{1,0:T(8,128)S(1)} custom-call(f32[8,128]{1,0:T(8,128)S(1)} %copy-done.7, f32[24,1024]{1,0:T(8,128)S(1)} %copy-done.6, f32[24,1024]{1,0:T(8,128)S(1)} %copy-done.6, f32[16,1024]{1,0:T(8,128)S(1)} %get-tuple-element.23.vec_ref.refs_7_.shift_ref), custom_call_target="tpu_custom_call" | custom-call | flops 4000000000 | bytes 1048576 | tf_op jit(solution)/shard_map/pallas_call | solution.py:142
  38.7 0.0 collective-permute-done.5.vec_ref
  38.7 2.3 %shard_map.115.refs_5_ = f32[16,1024]{1,0:T(8,128)S(1)} custom-call(f32[8,128]{1,0:T(8,128)S(1)} %copy-done.7, f32[24,1024]{1,0:T(8,128)S(1)} %copy-done.6, f32[24,1024]{1,0:T(8,128)S(1)} %collective-permute-done.2.other_ref.vec_ref, f32[16,1024]{1,0:T(8,128)S(1)} %collective-permute-done.5.vec_ref), custom_call_target="tpu_custom_call" | custom-call | flops 4000000000 | bytes 1048576 | tf_op jit(solution)/shard_map/pallas_call | solution.py:142
  41.0 6.5 %all-to-all-done.1.got_ref = f32[16,40,128]{2,1,0:T(8,128)S(1)} async-done(((f32[16,40,128]{2,1,0:T(8,128)}), f32[16,40,128]{2,1,0:T(8,128)S(1)}, u32[]{:S(2)}, u32[]{:S(2)}) %all-to-all-start.1) | async-done | bytes 327712 | tf_op jit(solution)/shard_map/all_to_all | solution.py:358
  47.5 1.6 %collective-permute-start.3 = (f32[24,128]{1,0:T(8,128)S(1)}, f32[24,128]{1,0:T(8,128)S(1)}, u32[]{:S(2)}, u32[]{:S(2)}) collective-permute-start(f32[24,128]{1,0:T(8,128)S(1)} %shard_map.111.refs_0_), channel_id=1, source_target_pairs={{0,16},{16,0},{1,17},{17,1},{2,18},{18,2},{3,19},{19,3},{4,20},{20... | collective-permute-start | bytes 36872 | tf_op jit(solution)/shard_map/ppermute | solution.py:405
  49.1 0.0 collective-permute-done.4.vec_ref
  49.1 2.3 %shard_map.114.refs_4_ = f32[16,1024]{1,0:T(8,128)S(1)} custom-call(f32[8,128]{1,0:T(8,128)S(1)} %copy-done.7, f32[24,1024]{1,0:T(8,128)S(1)} %copy-done.6, f32[24,1024]{1,0:T(8,128)S(1)} %collective-permute-done.1.other_ref.vec_ref, f32[16,1024]{1,0:T(8,128)S(1)} %collective-permute-done.4.vec_ref), custom_call_target="tpu_custom_call" | custom-call | flops 4000000000 | bytes 1048576 | tf_op jit(solution)/shard_map/pallas_call | solution.py:142
  51.3 0.5 shard_map.112.refs_2_
  51.8 0.0 collective-permute-done.3.refs_1_
  51.8 0.8 %shard_map.116 = (f32[16,1024]{1,0:T(8,128)S(1)}, f32[16,1024]{1,0:T(8,128)S(1)}, f32[16,128]{1,0:T(8,128)S(1)}, f32[32,1,128]{2,1,0:T(1,128)S(1)}) custom-call(f32[24,128]{1,0:T(8,128)S(1)} %shard_map.111.refs_0_, f32[24,128]{1,0:T(8,128)S(1)} %collective-permute-done.3.refs_1_, f32[16,128]{1,0:T(8,128)S(1)} %shard_map.112.refs_2_, ...), custom_call_target="tpu_custom_call" | custom-call | flops 1000000 | bytes 1048576 | tf_op jit(solution)/shard_map/pallas_call | solution.py:142
  52.6 9.5 %all_to_all.15.got_ref = f32[32,1,128]{2,1,0:T(1,128)S(1)} all-to-all(f32[32,1,128]{2,1,0:T(1,128)S(1)} %get-tuple-element.26), channel_id=1, replica_groups=mesh['grp'=2,'leaf'=16] {'grp','leaf'}, dimensions={0} | all-to-all | bytes 32768 | tf_op jit(solution)/shard_map/all_to_all | solution.py:358
  62.1 0.9 %shard_map.117 = (f32[16,1024]{1,0:T(8,128)}, f32[16,1024]{1,0:T(8,128)}) custom-call(f32[32,1,128]{2,1,0:T(1,128)S(1)} %all_to_all.15.got_ref, f32[16,128]{1,0:T(8,128)S(1)} %get-tuple-element.27.alpha_ref, f32[16,1024]{1,0:T(8,128)S(1)} %copy-done.1, f32[16,1024]{1,0:T(8,128)S(1)} %get-tuple-element.23.vec_ref.refs_7_.shift_ref, ...), custom_call_target="tpu_custom_call" | custom-call | flops 1000000 | bytes 1048576 | tf_op jit(solution)/shard_map/pallas_call | solution.py:142
  (1 shorter events, 0.0 us)
Async XLA Ops:
  2.9 12.5 %collective-permute-start.1 = (f32[24,1024]{1,0:T(8,128)}, f32[24,1024]{1,0:T(8,128)S(1)}, u32[]{:S(2)}, u32[]{:S(2)}) collective-permute-start(f32[24,1024]{1,0:T(8,128)} %get-tuple-element.19.own_ref.other_ref.vec_ref), channel_id=1, source_target_pairs={{0,1},{1,0},{2,3},{3,2},{4,5},{5,4},{6,7},{7,6},{8,9},{9,8},{10,11... | collective-permute-start | bytes 294920 | tf_op jit(solution)/shard_map/ppermute | solution.py:362
  3.5 14.2 %collective-permute-start.2 = (f32[24,1024]{1,0:T(8,128)}, f32[24,1024]{1,0:T(8,128)S(1)}, u32[]{:S(2)}, u32[]{:S(2)}) collective-permute-start(f32[24,1024]{1,0:T(8,128)} %get-tuple-element.19.own_ref.other_ref.vec_ref), channel_id=1, source_target_pairs={{1,2},{2,1},{3,4},{4,3},{5,6},{6,5},{7,8},{8,7},{9,10},{10,9},{11,... | collective-permute-start | bytes 294920 | tf_op jit(solution)/shard_map/ppermute | solution.py:362
  4.2 9.0 %copy-start.6 = (f32[24,1024]{1,0:T(8,128)S(1)}, f32[24,1024]{1,0:T(8,128)}, u32[]{:S(2)}) copy-start(f32[24,1024]{1,0:T(8,128)} %get-tuple-element.19.own_ref.other_ref.vec_ref) | copy-start | bytes 294916
  4.2 9.0 %copy-start.7 = (f32[8,128]{1,0:T(8,128)S(1)}, f32[8,128]{1,0:T(8,128)}, u32[]{:S(2)}) copy-start(f32[8,128]{1,0:T(8,128)} %get-tuple-element.18.weight_ref) | copy-start | bytes 12292
  4.2 20.0 %all-to-all-start = ((f32[16,40,128]{2,1,0:T(8,128)}), f32[16,40,128]{2,1,0:T(8,128)S(1)}, u32[]{:S(2)}, u32[]{:S(2)}) async-start(f32[16,40,128]{2,1,0:T(8,128)} %get-tuple-element.16.mine_ref), calls=%async_computation | async-start | bytes 655360 | tf_op jit(solution)/shard_map/all_to_all | solution.py:358
  17.7 6.5 %copy-start.5 = (s32[1,128]{1,0:T(1,128)S(1)}, s32[1,128]{1,0:T(1,128)}, u32[]{:S(2)}) copy-start(s32[1,128]{1,0:T(1,128)} %pick_ref.1) | copy-start | bytes 1540
  20.0 6.0 %copy-start.3 = (f32[16,40,128]{2,1,0:T(8,128)S(1)}, f32[16,40,128]{2,1,0:T(8,128)}, u32[]{:S(2)}) copy-start(f32[16,40,128]{2,1,0:T(8,128)} %get-tuple-element.16.mine_ref) | copy-start | bytes 983044
  24.4 3.8 %copy-start = (f32[1024,128]{1,0:T(8,128)S(1)}, f32[1024,128]{1,0:T(8,128)}, u32[]{:S(2)}) copy-start(f32[1024,128]{1,0:T(8,128)} %refs_10_.1) | copy-start | bytes 1572868
  24.5 3.8 %copy-start.1 = (f32[16,1024]{1,0:T(8,128)S(1)}, f32[16,1024]{1,0:T(8,128)}, u32[]{:S(2)}) copy-start(f32[16,1024]{1,0:T(8,128)} %rhs_ref.1) | copy-start | bytes 196612
  24.5 3.8 %copy-start.2 = (f32[1,128,128]{2,1,0:T(8,128)S(1)}, f32[1,128,128]{2,1,0:T(8,128)}, u32[]{:S(2)}) copy-start(f32[1,128,128]{2,1,0:T(8,128)} %refs_9_.3) | copy-start | bytes 196612
  24.5 3.8 %collective-permute-start = (f32[24,128]{1,0:T(8,128)S(1)}, f32[24,128]{1,0:T(8,128)S(1)}, u32[]{:S(2)}, u32[]{:S(2)}) collective-permute-start(f32[24,128]{1,0:T(8,128)S(1)} %shard_map.105.refs_0_), channel_id=1, source_target_pairs={{0,16},{16,0},{1,17},{17,1},{2,18},{18,2},{3,19},{19,3},{4,20},{20... | collective-permute-start | bytes 36872 | tf_op jit(solution)/shard_map/ppermute | solution.py:405
  26.0 2.2 %copy-start.4 = (f32[1024]{0:T(1024)S(1)}, f32[1024]{0:T(1024)}, u32[]{:S(2)}) copy-start(f32[1024]{0:T(1024)} %param.13) | copy-start | bytes 12292
  30.1 8.6 %collective-permute-start.5 = (f32[16,1024]{1,0:T(8,128)S(1)}, f32[16,1024]{1,0:T(8,128)S(1)}, u32[]{:S(2)}, u32[]{:S(2)}) collective-permute-start(f32[16,1024]{1,0:T(8,128)S(1)} %get-tuple-element.23.vec_ref.refs_7_.shift_ref), channel_id=1, source_target_pairs={{1,2},{2,1},{3,4},{4,3},{5,6},{6,5},{7,8},{8,7},{9,10},{10,9},{11,... | collective-permute-start | bytes 196616 | tf_op jit(solution)/shard_map/ppermute | solution.py:362
  30.7 18.3 %collective-permute-start.4 = (f32[16,1024]{1,0:T(8,128)S(1)}, f32[16,1024]{1,0:T(8,128)S(1)}, u32[]{:S(2)}, u32[]{:S(2)}) collective-permute-start(f32[16,1024]{1,0:T(8,128)S(1)} %get-tuple-element.23.vec_ref.refs_7_.shift_ref), channel_id=1, source_target_pairs={{0,1},{1,0},{2,3},{3,2},{4,5},{5,4},{6,7},{7,6},{8,9},{9,8},{10,11... | collective-permute-start | bytes 196616 | tf_op jit(solution)/shard_map/ppermute | solution.py:362
  31.8 15.7 %all-to-all-start.1 = ((f32[16,40,128]{2,1,0:T(8,128)}), f32[16,40,128]{2,1,0:T(8,128)S(1)}, u32[]{:S(2)}, u32[]{:S(2)}) async-start(f32[16,40,128]{2,1,0:T(8,128)} %get-tuple-element.20), calls=%async_computation.1 | async-start | bytes 655360 | tf_op jit(solution)/shard_map/all_to_all | solution.py:358
  47.5 4.3 %collective-permute-start.3 = (f32[24,128]{1,0:T(8,128)S(1)}, f32[24,128]{1,0:T(8,128)S(1)}, u32[]{:S(2)}, u32[]{:S(2)}) collective-permute-start(f32[24,128]{1,0:T(8,128)S(1)} %shard_map.111.refs_0_), channel_id=1, source_target_pairs={{0,16},{16,0},{1,17},{17,1},{2,18},{18,2},{3,19},{19,3},{4,20},{20... | collective-permute-start | bytes 36872 | tf_op jit(solution)/shard_map/ppermute | solution.py:405
where the time goes:
time: 63.3 us; the launch traced here: 62.9 us
  Pallas kernels  21.3 us (34%)
  starting transfers between devices  19.6 us (31%)
  waiting for transfers between devices  11.7 us (18%)
  blocking collectives  9.48 us (15%)
  between operations  0.77 us (1%)
    pallas_call x14, Pallas kernels, call(): pl.pallas_call(kernel, out_shape=[jax.ShapeDtypeStruct(s, d) for s, d in...  21.3 us
    all_to_all x2, starting transfers between devices, spread(): return lax.all_to_all(value, axis, 0, 0, tiled=True)  13.6 us
    all_to_all x2, waiting for transfers between devices, spread(): return lax.all_to_all(value, axis, 0, 0, tiled=True)  10.7 us
    all_to_all x1, blocking collectives, spread(): return lax.all_to_all(value, axis, 0, 0, tiled=True)  9.48 us
    ppermute x2, starting transfers between devices, exchange(): lax.ppermute(value, 'grp', [(i, (i + s) % groups) for i in range(groups)])  3.11 us
    ppermute x4, starting transfers between devices, pass_on(): return lax.ppermute(value, 'leaf', pairs)  2.9 us
  transfers between devices with their start and end apart: 8, of which 3 were waited for; matrix products, arithmetic and copies ran while one was open for 0% of the time, Pallas kernels for 24%

commit v1 on v0

--- a/solution.py
+++ b/solution.py
@@ -167,7 +167,7 @@
         copy.wait()
     dim, width = points_ref.shape
     rhs_rows = rhs_ref.shape[0]
-    _, rows, skel = send_ref.shape
+    rows, skel = send_ref.shape[1:]
     sub = lax.broadcasted_iota(jnp.int32, (dim, 1), 0)
     scale = jnp.zeros((dim, 1), F32)
     for d in range(dim):
@@ -213,23 +213,6 @@
         out_ref[:, cols] = fold(total) * weight
 
 
-def group_kernel(got_ref, pick_ref, out_ref, *, dim, rhs_rows):
-    boxes, rows, skel = got_ref.shape
-    start = dim + rhs_rows
-
-    def body(index, carry):
-        chosen, summed = carry
-        block = got_ref[index]
-        pick = lax.broadcasted_iota(jnp.int32, (skel, skel), 0) + index * skel == pick_ref[...]
-        pick = jnp.where(pick, 1.0, 0.0).astype(BF16)
-        return chosen + raw(triple(block[0:dim]), pick), summed + block[start:]
-
-    zero = (jnp.zeros((3 * dim, skel), F32), jnp.zeros((rows - start, skel), F32))
-    chosen, summed = each(boxes, body, zero)
-    out_ref[0:dim, :] = fold(chosen)
-    out_ref[dim:, :] = summed
-
-
 def box_chunks(boxes):
     step = min(boxes, 16)
     while boxes % step:
@@ -237,13 +220,38 @@
     return step, boxes // step
 
 
-def far_kernel(got_ref, mine_ref, high_ref, low_ref, out_ref, *, dim):
-    rhs_rows, skel = out_ref.shape
-    step, count = box_chunks(got_ref.shape[0])
-    left = stack_left(mine_ref[0, 0:dim, :])
+def picked(ref, pick_refs, swapped, dim, rhs_rows):
+    skel = ref.shape[2]
+    groups = len(pick_refs)
+    half = ref.shape[0] // groups
+    parity = lax.rem(lax.axis_index("leaf") + swapped, 2)
+    out = []
+    for shift, pick_ref in enumerate(pick_refs):
+        first = lax.rem(lax.axis_index("grp") + groups - shift, groups) * half
+
+        def body(index, carry, first=first, pick_ref=pick_ref):
+            chosen, summed = carry
+            block = ref[first + index]
+            place = lax.broadcasted_iota(jnp.int32, (skel, skel), 0)
+            pick = place + (2 * index + parity) * skel == pick_ref[...]
+            pick = jnp.where(pick, 1.0, 0.0).astype(BF16)
+            chosen = chosen + raw(triple(block[0:dim]), pick)
+            return chosen, summed + block[dim + rhs_rows : dim + 2 * rhs_rows]
+
+        zero = (jnp.zeros((3 * dim, skel), F32), jnp.zeros((rhs_rows, skel), F32))
+        chosen, summed = each(half, body, zero)
+        out.append(jnp.concatenate([fold(chosen), summed], axis=0))
+    return out
+
+
+def far_part(ref, groups, left, high_ref, low_ref, dim, rhs_rows):
+    skel = ref.shape[2]
+    half = ref.shape[0] // groups
+    first = lax.axis_index("grp") * half
+    step, count = box_chunks(half)
 
     def body(index, total):
-        blocks = [got_ref[index * step + j] for j in range(step)]
+        blocks = [ref[first + index * step + j] for j in range(step)]
         right = stack_right(jnp.concatenate([block[0:dim] for block in blocks], axis=1))
         coeff = jnp.concatenate([block[dim : dim + rhs_rows] for block in blocks], axis=1)
         high, low = split2(matern3(raw(left, right)))
@@ -251,69 +259,115 @@
         low_ref[index] = low
         return total + times_parts_t(coeff, high, low)
 
-    out_ref[...] = each(count, body, jnp.zeros((rhs_rows, skel), F32)) * THIRD
-
-
-def far_again_kernel(got_ref, high_ref, low_ref, out_ref):
-    rhs_rows, skel = out_ref.shape
-    step, count = box_chunks(got_ref.shape[0])
+    return each(count, body, jnp.zeros((rhs_rows, skel), F32))
+
+
+def far_again(ref, groups, high_ref, low_ref, rhs_rows):
+    skel = ref.shape[2]
+    half = ref.shape[0] // groups
+    first = lax.axis_index("grp") * half
+    step, count = box_chunks(half)
 
     def body(index, total):
-        blocks = [got_ref[index * step + j, 0:rhs_rows, :] for j in range(step)]
+        blocks = [ref[first + index * step + j, 0:rhs_rows, :] for j in range(step)]
         coeff = jnp.concatenate(blocks, axis=1)
         return total + times_parts_t(coeff, high_ref[index], low_ref[index])
 
-    out_ref[...] = each(count, body, jnp.zeros((rhs_rows, skel), F32)) * THIRD
-
-
-def sum_kernel(got_ref, out_ref):
-    start = got_ref.shape[1] - out_ref.shape[0]
-
-    def body(index, total):
-        return total + got_ref[index, start:, :]
-
-    out_ref[...] = each(got_ref.shape[0], body, jnp.zeros(out_ref.shape, F32))
-
-
-def first_image_kernel(*refs, dim, groups):
-    group_refs = refs[0:groups]
-    (far_ref, near_ref, near_a_ref, near_b_ref, rhs_ref, noise_ref, lift_ref, basis_ref,
-     shift_ref, send_ref, high_ref, low_ref) = refs[groups:]
-    rhs_rows = rhs_ref.shape[0]
-    _, rows, skel = send_ref.shape
-    left = stack_left(group_refs[0][0:dim, :])
-    right = stack_right(jnp.concatenate([ref[0:dim, :] for ref in group_refs], axis=1))
+    return each(count, body, jnp.zeros((rhs_rows, skel), F32))
+
+
+def group_sums(ref, groups, start):
+    half = ref.shape[0] // groups
+    out = []
+    for shift in range(groups):
+        first = lax.rem(lax.axis_index("grp") + groups - shift, groups) * half
+
+        def body(index, total, first=first):
+            return total + ref[first + index, start:, :]
+
+        out.append(each(half, body, jnp.zeros((ref.shape[1] - start, ref.shape[2]), F32)))
+    return out
+
+
+def half_kernel(*refs, groups):
+    got_ref = refs[0]
+    pick_refs = refs[1 : 1 + groups]
+    (mine_ref, near_ref, near_a_ref, near_b_ref, rhs_ref, noise_ref, basis_ref,
+     part_ref, left_ref, high_ref, low_ref, far_ref, base_ref, coeff_ref, gram_ref) = refs[1 + groups :]
+    rhs_rows, skel = coeff_ref.shape
+    dim = part_ref.shape[1] - rhs_rows
+    left = stack_left(mine_ref[0, 0:dim, :])
+    left_ref[...] = left
+    far_ref[...] = far_part(got_ref, groups, left, high_ref, low_ref, dim, rhs_rows)
+    for index, part in enumerate(picked(got_ref, pick_refs, 0, dim, rhs_rows)):
+        part_ref[index] = part
+    near = near_ref[...] + near_a_ref[...] + near_b_ref[...]
+    base = (noise_ref[...] - SHIFT) * rhs_ref[...] + near
+    base_ref[...] = base
+    basis = basis_ref[...]
+    both = pair(basis)
+    coeff_ref[...] = times(base, both)
+    flat = basis.T
+    square = raw(jnp.concatenate(split2(flat), axis=0), both)
+    gram_ref[...] = (
+        square[:skel, :skel] + square[:skel, skel:] + (square[skel:, :skel] + square[skel:, skel:])
+    )
+
+
+def first_image_kernel(*refs, groups):
+    got_ref = refs[0]
+    pick_refs = refs[1 : 1 + groups]
+    (part_ref, left_ref, far_ref, base_ref, coeff_ref, gram_ref, rhs_ref, lift_ref, basis_ref,
+     shift_ref, send_ref, top_high_ref, top_low_ref, high_ref, low_ref) = refs[1 + groups :]
+    rhs_rows, skel = coeff_ref.shape
+    dim = part_ref.shape[1] - rhs_rows
+    parts = picked(got_ref, pick_refs, 1, dim, rhs_rows)
+    parts = [part + part_ref[index] for index, part in enumerate(parts)]
+    far = far_ref[...] + far_part(got_ref, groups, left_ref[...], high_ref, low_ref, dim, rhs_rows)
+    left = stack_left(parts[0][0:dim])
+    right = stack_right(jnp.concatenate([part[0:dim] for part in parts], axis=1))
     high, low = split2(matern3(raw(left, right)))
-    high_ref[...] = high
-    low_ref[...] = low
-    start = dim + rhs_rows
-    coeff = jnp.concatenate([ref[dim:start, :] for ref in group_refs], axis=1)
-    top = times_parts_t(coeff, high, low) * THIRD
+    top_high_ref[...] = high
+    top_low_ref[...] = low
+    top = times_parts_t(jnp.concatenate([part[dim:] for part in parts], axis=1), high, low)
+    lift = pair(lift_ref[0])
+    row = (far + times_t(top, lift)) * THIRD
+    coeff = coeff_ref[...] + times(row, pair(gram_ref[...]))
+    lifted = times(coeff, lift)
     rhs = rhs_ref[...]
-    basis = pair(basis_ref[...])
-    lift = pair(lift_ref[0])
-    row = far_ref[...] + times_t(top, lift)
-    near = near_ref[...] + near_a_ref[...] + near_b_ref[...]
-    shift = (noise_ref[...] - SHIFT) * rhs + near + times_t(row, basis)
+    shift = base_ref[...] + times_t(row, pair(basis_ref[...]))
     shift_ref[...] = shift
-    coeff = times(shift, basis)
-    lifted = times(coeff, lift)
     total = to_row(row_sum(rhs * rhs))
     along = to_row(row_sum(rhs * shift))
-    rest = jnp.zeros((rows - 2 * rhs_rows - 2, skel), F32)
+    rest = jnp.zeros((send_ref.shape[1] - 2 * rhs_rows - 2, skel), F32)
     fill(send_ref, jnp.concatenate([coeff, lifted, total, along, rest], axis=0))
 
 
-def second_image_kernel(*refs, groups):
-    group_refs = refs[0:groups]
-    (far_ref, near_ref, near_a_ref, near_b_ref, rhs_ref, shift_ref, noise_ref,
-     lift_ref, basis_ref, high_ref, low_ref,
-     residual_ref, image_ref, alpha_ref, send_ref) = refs[groups:]
-    rhs_rows = rhs_ref.shape[0]
-    skel = lift_ref.shape[2]
-    coeff = jnp.concatenate([ref[0:rhs_rows, :] for ref in group_refs], axis=1)
-    top = times_parts_t(coeff, high_ref[...], low_ref[...]) * THIRD
-    sums = sum(ref[rhs_rows : rhs_rows + 8, :] for ref in group_refs)
+def half_again_kernel(
+    got_ref, near_ref, near_a_ref, near_b_ref, shift_ref, noise_ref, high_ref, low_ref,
+    part_ref, far_ref, base_ref,
+):
+    rhs_rows = far_ref.shape[0]
+    groups = part_ref.shape[0]
+    far_ref[...] = far_again(got_ref, groups, high_ref, low_ref, rhs_rows)
+    for index, part in enumerate(group_sums(got_ref, groups, rhs_rows)):
+        part_ref[index] = part
+    near = near_ref[...] + near_a_ref[...] + near_b_ref[...]
+    base_ref[...] = noise_ref[...] * shift_ref[...] + near
+
+
+def second_image_kernel(
+    got_ref, part_ref, far_ref, base_ref, high_ref, low_ref, top_high_ref, top_low_ref,
+    rhs_ref, shift_ref, lift_ref, basis_ref, residual_ref, image_ref, alpha_ref, send_ref,
+):
+    rhs_rows, skel = far_ref.shape
+    groups = part_ref.shape[0]
+    far = far_ref[...] + far_again(got_ref, groups, high_ref, low_ref, rhs_rows)
+    parts = group_sums(got_ref, groups, rhs_rows)
+    parts = [part + part_ref[index] for index, part in enumerate(parts)]
+    coeff = jnp.concatenate([part[0:rhs_rows] for part in parts], axis=1)
+    top = times_parts_t(coeff, top_high_ref[...], top_low_ref[...])
+    sums = sum(part[rhs_rows : rhs_rows + 8] for part in parts)
     total = to_column(sums[0:1], rhs_rows)
     along = to_column(sums[1:2], rhs_rows)
     curve = along + SHIFT * total
@@ -321,10 +375,9 @@
     keep = along / curve
     shift = shift_ref[...]
     rhs = rhs_ref[...]
-    row = far_ref[...] + times_t(top, pair(lift_ref[0]))
-    near = near_ref[...] + near_a_ref[...] + near_b_ref[...]
-    second = noise_ref[...] * shift + near + times_t(row, pair(basis_ref[...]))
+    row = (far + times_t(top, pair(lift_ref[0]))) * THIRD
     residual = keep * rhs - alpha * shift
+    second = base_ref[...] + times_t(row, pair(basis_ref[...]))
     image = keep * (shift + SHIFT * rhs) - alpha * second
     residual_ref[...] = residual
     image_ref[...] = image
@@ -354,12 +407,14 @@
     out_ref[...] = residual - step * (image_ref[...] + ratio * image)
 
 
-def spread(value, axis):
-    return lax.all_to_all(value, axis, 0, 0, tiled=True)
-
-
-def pass_on(value, pairs):
-    return lax.ppermute(value, "leaf", pairs)
+def spread(value, members=None):
+    return lax.all_to_all(
+        value, ("grp", "leaf"), 0, 0, tiled=True, axis_index_groups=members
+    )
+
+
+def pass_on(value, pairs, axis="leaf"):
+    return lax.ppermute(value, axis, pairs)
 
 
 def local(points, rhs, basis, transfer, noise, inv_scale, links, leaf_skel, group_skel):
@@ -368,27 +423,41 @@
     skel = basis.shape[1]
     boxes = lax.axis_size("leaf")
     groups = lax.axis_size("grp")
+    half = boxes // 2
+    assert boxes == 2 * half
     noise = noise[None, :]
-    pairs_a = [(i, i ^ 1) for i in range(boxes) if (i ^ 1) < boxes]
-    pairs_b = [(i, ((i + 1) ^ 1) - 1) for i in range(boxes) if 0 <= ((i + 1) ^ 1) - 1 < boxes]
+    pairs_a = [(i, i ^ 1) for i in range(boxes)]
+    pairs_b = [(i, ((i + 1) ^ 1) - 1) for i in range(1, boxes - 1)]
+    members = [[2 * i + c for i in range(groups * half)] for c in range(2)]
     wide = (rhs_rows, width)
     small = (rhs_rows, skel)
-    step, count = box_chunks(boxes)
+    step, count = box_chunks(half)
+    far_shape = ((count, skel, step * skel), BF16)
+    top_shape = ((skel, groups * skel), BF16)
 
     rows = -(-(dim + 2 * rhs_rows) // 8) * 8
+    rows_next = -(-(2 * rhs_rows + 2) // 8) * 8
+    room = 8 + (2 * groups * half * rows * skel * 4 + 4 * half * skel * skel * 4) // MIB
     inputs = [points, rhs, basis, transfer, noise, inv_scale, links, leaf_skel]
     scratch = [pltpu.VMEM(value.shape, value.dtype) for value in inputs]
     for index in (5, 6):
         scratch[index] = pltpu.SMEM(inputs[index].shape, inputs[index].dtype)
     beside, send, weight = call(
         prepare_kernel,
-        [((dim + rhs_rows, width), F32), ((boxes, rows, skel), F32), ((8, skel), F32)],
+        [((dim + rhs_rows, width), F32), ((groups * half, rows, skel), F32), ((8, skel), F32)],
         inputs, space=pltpu.HBM, scratch=scratch + [pltpu.SemaphoreType.DMA((8,))],
         limit=60,
     )
-    got = spread(send, "leaf")
+    got = spread(send, members)
     beside_a = pass_on(beside, pairs_a)
     beside_b = pass_on(beside, pairs_b)
+    picks = [group_skel] + [
+        pass_on(
+            group_skel, [(i, (i + s) % groups) for i in range(groups)],
+            "grp",
+        )
+        for s in range(1, groups)
+    ]
 
     def near_part(other, vec, kind):
         return call(
@@ -399,46 +468,41 @@
     near = near_part(beside, beside, 0)
     near_a = near_part(beside_a, beside_a, 1)
     near_b = near_part(beside_b, beside_b, 2)
-
-    def exchange(value):
-        return [value] + [
-            lax.ppermute(value, "grp", [(i, (i + s) % groups) for i in range(groups)])
-            for s in range(1, groups)
-        ]
-
-    (mine,) = call(
-        functools.partial(group_kernel, dim=dim, rhs_rows=rhs_rows),
-        [((rows - rhs_rows, skel), F32)], [got, group_skel],
-    )
-    parts = exchange(mine)
-    far_shape = ((count, skel, step * skel), BF16)
-    far_high, far_low, far = call(
-        functools.partial(far_kernel, dim=dim), [far_shape, far_shape, (small, F32)], [got, send],
-        limit=16, flops=10**9,
-    )
-    rows_next = -(-(2 * rhs_rows + 2) // 8) * 8
-    top_shape = ((skel, groups * skel), BF16)
-    shift, send, top_high, top_low = call(
-        functools.partial(first_image_kernel, dim=dim, groups=groups),
-        [(wide, F32), ((boxes, rows_next, skel), F32), top_shape, top_shape],
-        [*parts, far, near, near_a, near_b, rhs, noise, transfer, basis],
-    )
-    got = spread(send, "leaf")
+    peer = pass_on(got, pairs_a)
+    part, left, high, low, far, base, coeff, gram = call(
+        functools.partial(half_kernel, groups=groups),
+        [((groups, dim + rhs_rows, skel), F32), ((skel, skel), BF16), far_shape, far_shape,
+         (small, F32), (wide, F32), (small, F32), ((skel, skel), F32)],
+        [got, *picks, send, near, near_a, near_b, rhs, noise, basis],
+        limit=room, flops=10**9,
+    )
+    shift, send, top_high, top_low, peer_high, peer_low = call(
+        functools.partial(first_image_kernel, groups=groups),
+        [(wide, F32), ((groups * half, rows_next, skel), F32), top_shape, top_shape,
+         far_shape, far_shape],
+        [peer, *picks, part, left, far, base, coeff, gram, rhs, transfer, basis],
+        limit=room,
+    )
+    got = spread(send, members)
     shift_a = pass_on(shift, pairs_a)
     shift_b = pass_on(shift, pairs_b)
     near = near_part(beside, shift, 0)
     near_a = near_part(beside_a, shift_a, 1)
     near_b = near_part(beside_b, shift_b, 2)
-    (mine,) = call(sum_kernel, [((rows_next - rhs_rows, skel), F32)], [got])
-    parts = exchange(mine)
-    (far,) = call(far_again_kernel, [(small, F32)], [got, far_high, far_low], flops=10**8)
+    peer = pass_on(got, pairs_a)
+    part, far, base = call(
+        half_again_kernel,
+        [((groups, rows_next - rhs_rows, skel), F32), (small, F32), (wide, F32)],
+        [got, near, near_a, near_b, shift, noise, high, low],
+        limit=room, flops=10**9,
+    )
     residual, image, alpha, send = call(
-        functools.partial(second_image_kernel, groups=groups),
+        second_image_kernel,
         [(wide, F32), (wide, F32), (small, F32), ((boxes * groups, 1, skel), F32)],
-        [*parts, far, near, near_a, near_b, rhs, shift, noise, transfer, basis,
-         top_high, top_low],
-    )
-    got = spread(send, ("grp", "leaf"))
+        [peer, part, far, base, peer_high, peer_low, top_high, top_low, rhs, shift, transfer, basis],
+        limit=room,
+    )
+    got = spread(send)
     return tuple(
         call(
             finish_kernel, [(wide, F32), (wide, F32)],

time: 63.3 us -> 64 us (1.011)
  blocking collectives: 9.48 us -> 12.1 us
  waiting for transfers between devices: 11.7 us -> 9.9 us
    all_to_all x2, starting transfers between devices: 13.6 us -> 8.66 us  [spread(): lax.all_to_all(value, ('grp', 'leaf'), 0, 0, tiled=True, axis_index_group...]
    ppermute x6 -> x7, starting transfers between devices: 6.02 us -> 10.6 us  [pass_on(): return lax.ppermute(value, axis, pairs)]
    all_to_all x1, blocking collectives: 9.48 us -> 12.1 us  [spread(): lax.all_to_all(value, ('grp', 'leaf'), 0, 0, tiled=True, axis_index_group...]
    ppermute x6 -> x7, waiting for transfers between devices: 1.09 us -> 0.02 us  [pass_on(): return lax.ppermute(value, axis, pairs)]
    all_to_all x2, waiting for transfers between devices: 10.7 us -> 9.88 us  [spread(): lax.all_to_all(value, ('grp', 'leaf'), 0, 0, tiled=True, axis_index_group...]
    pallas_call x14 -> x12, Pallas kernels: 21.3 us -> 21.5 us  [call(): pl.pallas_call(kernel, out_shape=[jax.ShapeDtypeStruct(s, d) for s, d in...]
  transfers between devices with their start and end apart: 8 -> 9, of which waited for: 3 -> 2; matrix products, arithmetic and copies ran while one was open for 0% -> 0% of each run, Pallas kernels for 24% -> 24%
where the time goes in v1:
time: 64 us; the launch traced here: 63.6 us
  Pallas kernels  21.5 us (34%)
  starting transfers between devices  19.3 us (30%)
  blocking collectives  12.1 us (19%)
  waiting for transfers between devices  9.9 us (15%)
  between operations  0.79 us (1%)
    pallas_call x12, Pallas kernels, call(): pl.pallas_call(kernel, out_shape=[jax.ShapeDtypeStruct(s, d) for s, d in...  21.5 us
    all_to_all x1, blocking collectives, spread(): lax.all_to_all(value, ('grp', 'leaf'), 0, 0, tiled=True, axis_index_group...  12.1 us
    ppermute x7, starting transfers between devices, pass_on(): return lax.ppermute(value, axis, pairs)  10.6 us
    all_to_all x2, waiting for transfers between devices, spread(): lax.all_to_all(value, ('grp', 'leaf'), 0, 0, tiled=True, axis_index_group...  9.88 us
    all_to_all x2, starting transfers between devices, spread(): lax.all_to_all(value, ('grp', 'leaf'), 0, 0, tiled=True, axis_index_group...  8.66 us
  transfers between devices with their start and end apart: 9, of which 2 were waited for; matrix products, arithmetic and copies ran while one was open for 0% of the time, Pallas kernels for 24%

profile of v1, /device:TPU:0, one launch (start us, length us, event | category | flops | bytes accessed | tf_op | source)
XLA Modules:
  0.0 63.6 jit_solution(5114631408210068492)
XLA Ops:
  0.6 2.3 %shard_map.104 = (f32[24,1024]{1,0:T(8,128)}, f32[16,40,128]{2,1,0:T(8,128)}, f32[8,128]{1,0:T(8,128)}) custom-call(f32[8,1024]{1,0:T(8,128)} %points_hbm.1, f32[16,1024]{1,0:T(8,128)} %rhs_ref.3, f32[1024,128]{1,0:T(8,128)} %basis_ref.1, f32[1,128,128]{2,1,0:T(8,128)} %lift_ref.1, f32[1,1024]{1,0:T(1,128)} %bitcast.1, f32[8]{0:T(128)} %scale_hbm.1, ...), custom_call_target="tpu_custom_call" | custom-call | flops 1000000 | bytes 1048576 | tf_op jit(solution)/shard_map/pallas_call | solution.py:142
  2.9 0.0 copy-start.5
  2.9 0.7 %collective-permute-start.3 = (f32[24,1024]{1,0:T(8,128)}, f32[24,1024]{1,0:T(8,128)S(1)}, u32[]{:S(2)}, u32[]{:S(2)}) collective-permute-start(f32[24,1024]{1,0:T(8,128)} %get-tuple-element.28.own_ref.other_ref.vec_ref), channel_id=1, source_target_pairs={{1,2},{2,1},{3,4},{4,3},{5,6},{6,5},{7,8},{8,7},{9,10},{10,9},{11,... | collective-permute-start | bytes 294920 | tf_op jit(solution)/shard_map/ppermute | solution.py:417
  3.6 4.4 %collective-permute-start.2 = (f32[24,1024]{1,0:T(8,128)}, f32[24,1024]{1,0:T(8,128)S(1)}, u32[]{:S(2)}, u32[]{:S(2)}) collective-permute-start(f32[24,1024]{1,0:T(8,128)} %get-tuple-element.28.own_ref.other_ref.vec_ref), channel_id=1, source_target_pairs={{0,1},{1,0},{2,3},{3,2},{4,5},{5,4},{6,7},{7,6},{8,9},{9,8},{10,11... | collective-permute-start | bytes 294920 | tf_op jit(solution)/shard_map/ppermute | solution.py:417
  8.0 0.0 copy-done.5
  8.0 1.5 %collective-permute-start.1 = (s32[1,128]{1,0:T(1,128)S(1)}, s32[1,128]{1,0:T(1,128)S(1)}, u32[]{:S(2)}, u32[]{:S(2)}) collective-permute-start(s32[1,128]{1,0:T(1,128)S(1)} %copy-done.5), channel_id=1, source_target_pairs={{0,16},{16,0},{1,17},{17,1},{2,18},{18,2},{3,19},{19,3},{4,20},{20... | collective-permute-start | bytes 1544 | tf_op jit(solution)/shard_map/ppermute | solution.py:417
  9.5 0.0 copy-start.6
  9.5 0.0 copy-start.7
  9.5 5.1 %all-to-all-start = ((f32[16,40,128]{2,1,0:T(8,128)}), f32[16,40,128]{2,1,0:T(8,128)S(1)}, u32[]{:S(2)}, u32[]{:S(2)}) async-start(f32[16,40,128]{2,1,0:T(8,128)} %get-tuple-element.26.refs_3_), calls=%async_computation | async-start | bytes 655360 | tf_op jit(solution)/shard_map/all_to_all | solution.py:411
  14.7 0.0 copy-done.6
  14.7 0.0 copy-done.7
  14.7 2.3 %shard_map.105.refs_4_ = f32[16,1024]{1,0:T(8,128)S(1)} custom-call(f32[8,128]{1,0:T(8,128)S(1)} %copy-done.7, f32[24,1024]{1,0:T(8,128)S(1)} %copy-done.6, f32[24,1024]{1,0:T(8,128)S(1)} %copy-done.6, f32[24,1024]{1,0:T(8,128)S(1)} %copy-done.6), custom_call_target="tpu_custom_call" | custom-call | flops 4000000000 | bytes 1048576 | tf_op jit(solution)/shard_map/pallas_call | solution.py:142
  17.0 0.0 collective-permute-done.3.other_ref.vec_ref
  17.0 2.3 %shard_map.107.refs_6_ = f32[16,1024]{1,0:T(8,128)S(1)} custom-call(f32[8,128]{1,0:T(8,128)S(1)} %copy-done.7, f32[24,1024]{1,0:T(8,128)S(1)} %copy-done.6, f32[24,1024]{1,0:T(8,128)S(1)} %collective-permute-done.3.other_ref.vec_ref, f32[24,1024]{1,0:T(8,128)S(1)} %collective-permute-done.3.other_ref.vec_ref), custom_call_target="tpu_custom_call" | custom-call | flops 4000000000 | bytes 1048576 | tf_op jit(solution)/shard_map/pallas_call | solution.py:142
  19.3 0.0 copy-start
  19.3 0.0 copy-start.1
  19.3 0.0 copy-start.3
  19.3 0.0 copy-start.4
  19.3 6.6 %all-to-all-done.refs_0_ = f32[16,40,128]{2,1,0:T(8,128)S(1)} async-done(((f32[16,40,128]{2,1,0:T(8,128)}), f32[16,40,128]{2,1,0:T(8,128)S(1)}, u32[]{:S(2)}, u32[]{:S(2)}) %all-to-all-start) | async-done | bytes 327712 | tf_op jit(solution)/shard_map/all_to_all | solution.py:411
  25.9 0.0 collective-permute-start
  25.9 0.0 collective-permute-done.2.other_ref.vec_ref
  26.0 2.3 %shard_map.106.refs_5_ = f32[16,1024]{1,0:T(8,128)S(1)} custom-call(f32[8,128]{1,0:T(8,128)S(1)} %copy-done.7, f32[24,1024]{1,0:T(8,128)S(1)} %copy-done.6, f32[24,1024]{1,0:T(8,128)S(1)} %collective-permute-done.2.other_ref.vec_ref, f32[24,1024]{1,0:T(8,128)S(1)} %collective-permute-done.2.other_ref.vec_ref), custom_call_target="tpu_custom_call" | custom-call | flops 4000000000 | bytes 1048576 | tf_op jit(solution)/shard_map/pallas_call | solution.py:142
  28.2 0.0 copy-start.2
  28.2 0.0 collective-permute-done.1.refs_2_
  28.2 0.0 copy-done
  28.3 0.0 copy-done.1
  28.3 0.0 copy-done.3
  28.3 0.0 copy-done.4
  28.3 1.0 %shard_map.108 = (f32[2,24,128]{2,1,0:T(8,128)S(1)}, bf16[128,128]{1,0:T(8,128)(2,1)S(1)}, bf16[1,128,1024]{2,1,0:T(8,128)(2,1)S(1)}, bf16[1,128,1024]{2,1,0:T(8...) custom-call(f32[16,40,128]{2,1,0:T(8,128)S(1)} %all-to-all-done.refs, ...), custom_call_target="tpu_custom_call" | custom-call | flops 1000000000 | bytes 1048576 | tf_op jit(solution)/shard_map/pallas_call | solution.py:142
  29.3 0.0 collective-permute-done.refs_0_
  29.4 0.0 copy-done.2
  29.4 2.3 %shard_map.109 = (f32[16,1024]{1,0:T(8,128)S(1)}, f32[16,40,128]{2,1,0:T(8,128)}, bf16[128,256]{1,0:T(8,128)(2,1)S(1)}, bf16[128,256]{1,0:T(8,128)(2,1)S(1)}, bf...) custom-call(f32[16,40,128]{2,1,0:T(8,128)S(1)} %collective-permute-done.refs_0_, ...), custom_call_target="tpu_custom_call" | custom-call | flops 1000000 | bytes 1048576 | tf_op jit(solution)/shard_map/pallas_call | solution.py:142
  31.6 3.5 %all-to-all-start.1 = ((f32[16,40,128]{2,1,0:T(8,128)}), f32[16,40,128]{2,1,0:T(8,128)S(1)}, u32[]{:S(2)}, u32[]{:S(2)}) async-start(f32[16,40,128]{2,1,0:T(8,128)} %get-tuple-element.35), calls=%async_computation.1 | async-start | bytes 655360 | tf_op jit(solution)/shard_map/all_to_all | solution.py:411
  35.2 0.8 %collective-permute-start.6 = (f32[16,1024]{1,0:T(8,128)S(1)}, f32[16,1024]{1,0:T(8,128)S(1)}, u32[]{:S(2)}, u32[]{:S(2)}) collective-permute-start(f32[16,1024]{1,0:T(8,128)S(1)} %get-tuple-element.36.vec_ref.shift_ref), channel_id=1, source_target_pairs={{1,2},{2,1},{3,4},{4,3},{5,6},{6,5},{7,8},{8,7},{9,10},{10,9},{11,... | collective-permute-start | bytes 196616 | tf_op jit(solution)/shard_map/ppermute | solution.py:417
  36.0 2.3 %shard_map.110.near_ref = f32[16,1024]{1,0:T(8,128)S(1)} custom-call(f32[8,128]{1,0:T(8,128)S(1)} %copy-done.7, f32[24,1024]{1,0:T(8,128)S(1)} %copy-done.6, f32[24,1024]{1,0:T(8,128)S(1)} %copy-done.6, f32[16,1024]{1,0:T(8,128)S(1)} %get-tuple-element.36.vec_ref.shift_ref), custom_call_target="tpu_custom_call" | custom-call | flops 4000000000 | bytes 1048576 | tf_op jit(solution)/shard_map/pallas_call | solution.py:142
  38.3 3.2 %collective-permute-start.5 = (f32[16,1024]{1,0:T(8,128)S(1)}, f32[16,1024]{1,0:T(8,128)S(1)}, u32[]{:S(2)}, u32[]{:S(2)}) collective-permute-start(f32[16,1024]{1,0:T(8,128)S(1)} %get-tuple-element.36.vec_ref.shift_ref), channel_id=1, source_target_pairs={{0,1},{1,0},{2,3},{3,2},{4,5},{5,4},{6,7},{7,6},{8,9},{9,8},{10,11... | collective-permute-start | bytes 196616 | tf_op jit(solution)/shard_map/ppermute | solution.py:417
  41.5 0.0 collective-permute-done.6.vec_ref
  41.5 2.3 %shard_map.112.near_b_ref = f32[16,1024]{1,0:T(8,128)S(1)} custom-call(f32[8,128]{1,0:T(8,128)S(1)} %copy-done.7, f32[24,1024]{1,0:T(8,128)S(1)} %copy-done.6, f32[24,1024]{1,0:T(8,128)S(1)} %collective-permute-done.3.other_ref.vec_ref, f32[16,1024]{1,0:T(8,128)S(1)} %collective-permute-done.6.vec_ref), custom_call_target="tpu_custom_call" | custom-call | flops 4000000000 | bytes 1048576 | tf_op jit(solution)/shard_map/pallas_call | solution.py:142
  43.8 3.2 %all-to-all-done.1.got_ref = f32[16,40,128]{2,1,0:T(8,128)S(1)} async-done(((f32[16,40,128]{2,1,0:T(8,128)}), f32[16,40,128]{2,1,0:T(8,128)S(1)}, u32[]{:S(2)}, u32[]{:S(2)}) %all-to-all-start.1) | async-done | bytes 327712 | tf_op jit(solution)/shard_map/all_to_all | solution.py:411
  47.0 0.0 collective-permute-start.4
  47.0 0.0 collective-permute-done.5.vec_ref
  47.0 2.3 %shard_map.111.near_a_ref = f32[16,1024]{1,0:T(8,128)S(1)} custom-call(f32[8,128]{1,0:T(8,128)S(1)} %copy-done.7, f32[24,1024]{1,0:T(8,128)S(1)} %copy-done.6, f32[24,1024]{1,0:T(8,128)S(1)} %collective-permute-done.2.other_ref.vec_ref, f32[16,1024]{1,0:T(8,128)S(1)} %collective-permute-done.5.vec_ref), custom_call_target="tpu_custom_call" | custom-call | flops 4000000000 | bytes 1048576 | tf_op jit(solution)/shard_map/pallas_call | solution.py:142
  49.3 0.3 shard_map.113
  49.6 0.0 collective-permute-done.4.got_ref
  49.6 1.1 %shard_map.114 = (f32[16,1024]{1,0:T(8,128)S(1)}, f32[16,1024]{1,0:T(8,128)S(1)}, f32[16,128]{1,0:T(8,128)S(1)}, f32[32,1,128]{2,1,0:T(1,128)S(1)}) custom-call(f32[16,40,128]{2,1,0:T(8,128)S(1)} %collective-permute-done.4.got_ref, f32[2,24,128]{2,1,0:T(8,128)S(1)} %get-tuple-element.39.part_ref, f32[16,128]{1,0:T(8,128)S(1)} %get-tuple-element.40.far_ref, ...), custom_call_target="tpu_custom_call" | custom-call | flops 1000000 | bytes 1048576 | tf_op jit(solution)/shard_map/pallas_call | solution.py:142
  50.7 12.1 %all_to_all.15.got_ref = f32[32,1,128]{2,1,0:T(1,128)S(1)} all-to-all(f32[32,1,128]{2,1,0:T(1,128)S(1)} %get-tuple-element.46), channel_id=1, replica_groups=mesh['grp'=2,'leaf'=16] {'grp','leaf'}, dimensions={0} | all-to-all | bytes 32768 | tf_op jit(solution)/shard_map/all_to_all | solution.py:411
  62.7 0.9 %shard_map.115 = (f32[16,1024]{1,0:T(8,128)}, f32[16,1024]{1,0:T(8,128)}) custom-call(f32[32,1,128]{2,1,0:T(1,128)S(1)} %all_to_all.15.got_ref, f32[16,128]{1,0:T(8,128)S(1)} %get-tuple-element.47.alpha_ref, f32[16,1024]{1,0:T(8,128)S(1)} %copy-done.1, f32[16,1024]{1,0:T(8,128)S(1)} %get-tuple-element.36.vec_ref.shift_ref, ...), custom_call_target="tpu_custom_call" | custom-call | flops 1000000 | bytes 1048576 | tf_op jit(solution)/shard_map/pallas_call | solution.py:142
Async XLA Ops:
  2.9 5.1 %copy-start.5 = (s32[1,128]{1,0:T(1,128)S(1)}, s32[1,128]{1,0:T(1,128)}, u32[]{:S(2)}) copy-start(s32[1,128]{1,0:T(1,128)} %refs_1_.3) | copy-start | bytes 1540
  2.9 14.0 %collective-permute-start.3 = (f32[24,1024]{1,0:T(8,128)}, f32[24,1024]{1,0:T(8,128)S(1)}, u32[]{:S(2)}, u32[]{:S(2)}) collective-permute-start(f32[24,1024]{1,0:T(8,128)} %get-tuple-element.28.own_ref.other_ref.vec_ref), channel_id=1, source_target_pairs={{1,2},{2,1},{3,4},{4,3},{5,6},{6,5},{7,8},{8,7},{9,10},{10,9},{11,... | collective-permute-start | bytes 294920 | tf_op jit(solution)/shard_map/ppermute | solution.py:417
  3.6 22.3 %collective-permute-start.2 = (f32[24,1024]{1,0:T(8,128)}, f32[24,1024]{1,0:T(8,128)S(1)}, u32[]{:S(2)}, u32[]{:S(2)}) collective-permute-start(f32[24,1024]{1,0:T(8,128)} %get-tuple-element.28.own_ref.other_ref.vec_ref), channel_id=1, source_target_pairs={{0,1},{1,0},{2,3},{3,2},{4,5},{5,4},{6,7},{7,6},{8,9},{9,8},{10,11... | collective-permute-start | bytes 294920 | tf_op jit(solution)/shard_map/ppermute | solution.py:417
  8.0 20.2 %collective-permute-start.1 = (s32[1,128]{1,0:T(1,128)S(1)}, s32[1,128]{1,0:T(1,128)S(1)}, u32[]{:S(2)}, u32[]{:S(2)}) collective-permute-start(s32[1,128]{1,0:T(1,128)S(1)} %copy-done.5), channel_id=1, source_target_pairs={{0,16},{16,0},{1,17},{17,1},{2,18},{18,2},{3,19},{19,3},{4,20},{20... | collective-permute-start | bytes 1544 | tf_op jit(solution)/shard_map/ppermute | solution.py:417
  9.5 5.1 %copy-start.6 = (f32[24,1024]{1,0:T(8,128)S(1)}, f32[24,1024]{1,0:T(8,128)}, u32[]{:S(2)}) copy-start(f32[24,1024]{1,0:T(8,128)} %get-tuple-element.28.own_ref.other_ref.vec_ref) | copy-start | bytes 294916
  9.5 5.1 %copy-start.7 = (f32[8,128]{1,0:T(8,128)S(1)}, f32[8,128]{1,0:T(8,128)}, u32[]{:S(2)}) copy-start(f32[8,128]{1,0:T(8,128)} %get-tuple-element.27.weight_ref) | copy-start | bytes 12292
  9.5 16.4 %all-to-all-start = ((f32[16,40,128]{2,1,0:T(8,128)}), f32[16,40,128]{2,1,0:T(8,128)S(1)}, u32[]{:S(2)}, u32[]{:S(2)}) async-start(f32[16,40,128]{2,1,0:T(8,128)} %get-tuple-element.26.refs_3_), calls=%async_computation | async-start | bytes 655360 | tf_op jit(solution)/shard_map/all_to_all | solution.py:411
  19.3 9.0 %copy-start = (f32[1024,128]{1,0:T(8,128)S(1)}, f32[1024,128]{1,0:T(8,128)}, u32[]{:S(2)}) copy-start(f32[1024,128]{1,0:T(8,128)} %basis_ref.1) | copy-start | bytes 1572868
  19.3 9.0 %copy-start.1 = (f32[16,1024]{1,0:T(8,128)S(1)}, f32[16,1024]{1,0:T(8,128)}, u32[]{:S(2)}) copy-start(f32[16,1024]{1,0:T(8,128)} %rhs_ref.3) | copy-start | bytes 196612
  19.3 9.0 %copy-start.3 = (f32[16,40,128]{2,1,0:T(8,128)S(1)}, f32[16,40,128]{2,1,0:T(8,128)}, u32[]{:S(2)}) copy-start(f32[16,40,128]{2,1,0:T(8,128)} %get-tuple-element.26.refs_3_) | copy-start | bytes 983044
  19.3 9.0 %copy-start.4 = (f32[1024]{0:T(1024)S(1)}, f32[1024]{0:T(1024)}, u32[]{:S(2)}) copy-start(f32[1024]{0:T(1024)} %param.13) | copy-start | bytes 12292
  25.9 3.4 %collective-permute-start = (f32[16,40,128]{2,1,0:T(8,128)S(1)}, f32[16,40,128]{2,1,0:T(8,128)S(1)}, u32[]{:S(2)}, u32[]{:S(2)}) collective-permute-start(f32[16,40,128]{2,1,0:T(8,128)S(1)} %all-to-all-done.refs_0_), channel_id=1, source_target_pairs={{0,1},{1,0},{2,3},{3,2},{4,5},{5,4},{6,7},{7,6},{8,9},{9,8},{10,11... | collective-permute-start | bytes 983048 | tf_op jit(solution)/shard_map/ppermute | solution.py:417
  28.2 1.1 %copy-start.2 = (f32[1,128,128]{2,1,0:T(8,128)S(1)}, f32[1,128,128]{2,1,0:T(8,128)}, u32[]{:S(2)}) copy-start(f32[1,128,128]{2,1,0:T(8,128)} %lift_ref.1) | copy-start | bytes 196612
  31.6 15.4 %all-to-all-start.1 = ((f32[16,40,128]{2,1,0:T(8,128)}), f32[16,40,128]{2,1,0:T(8,128)S(1)}, u32[]{:S(2)}, u32[]{:S(2)}) async-start(f32[16,40,128]{2,1,0:T(8,128)} %get-tuple-element.35), calls=%async_computation.1 | async-start | bytes 655360 | tf_op jit(solution)/shard_map/all_to_all | solution.py:411
  35.2 6.3 %collective-permute-start.6 = (f32[16,1024]{1,0:T(8,128)S(1)}, f32[16,1024]{1,0:T(8,128)S(1)}, u32[]{:S(2)}, u32[]{:S(2)}) collective-permute-start(f32[16,1024]{1,0:T(8,128)S(1)} %get-tuple-element.36.vec_ref.shift_ref), channel_id=1, source_target_pairs={{1,2},{2,1},{3,4},{4,3},{5,6},{6,5},{7,8},{8,7},{9,10},{10,9},{11,... | collective-permute-start | bytes 196616 | tf_op jit(solution)/shard_map/ppermute | solution.py:417
  38.3 8.7 %collective-permute-start.5 = (f32[16,1024]{1,0:T(8,128)S(1)}, f32[16,1024]{1,0:T(8,128)S(1)}, u32[]{:S(2)}, u32[]{:S(2)}) collective-permute-start(f32[16,1024]{1,0:T(8,128)S(1)} %get-tuple-element.36.vec_ref.shift_ref), channel_id=1, source_target_pairs={{0,1},{1,0},{2,3},{3,2},{4,5},{5,4},{6,7},{7,6},{8,9},{9,8},{10,11... | collective-permute-start | bytes 196616 | tf_op jit(solution)/shard_map/ppermute | solution.py:417
  47.0 2.6 %collective-permute-start.4 = (f32[16,40,128]{2,1,0:T(8,128)S(1)}, f32[16,40,128]{2,1,0:T(8,128)S(1)}, u32[]{:S(2)}, u32[]{:S(2)}) collective-permute-start(f32[16,40,128]{2,1,0:T(8,128)S(1)} %all-to-all-done.1.got_ref), channel_id=1, source_target_pairs={{0,1},{1,0},{2,3},{3,2},{4,5},{5,4},{6,7},{7,6},{8,9},{9,8},{10,11... | collective-permute-start | bytes 983048 | tf_op jit(solution)/shard_map/ppermute | solution.py:417

commit v2 on v1

--- a/solution.py
+++ b/solution.py
@@ -151,19 +151,19 @@
 
 
 def prepare_kernel(
-    points_hbm, rhs_hbm, basis_hbm, lift_hbm, noise_hbm, scale_hbm, links_hbm, skel_hbm,
+    points_hbm, rhs_hbm, basis_hbm, lift_hbm, scale_hbm, links_hbm, skel_hbm,
     beside_ref, send_ref, weight_ref,
-    points_ref, rhs_ref, basis_ref, lift_ref, noise_ref, scale_ref, links_ref, skel_ref, sems,
+    points_ref, rhs_ref, basis_ref, lift_ref, scale_ref, links_ref, skel_ref, sems,
 ):
-    sources = (points_hbm, scale_hbm, links_hbm, rhs_hbm, basis_hbm, skel_hbm, lift_hbm, noise_hbm)
-    targets = (points_ref, scale_ref, links_ref, rhs_ref, basis_ref, skel_ref, lift_ref, noise_ref)
+    sources = (points_hbm, scale_hbm, links_hbm, rhs_hbm, skel_hbm, basis_hbm, lift_hbm)
+    targets = (points_ref, scale_ref, links_ref, rhs_ref, skel_ref, basis_ref, lift_ref)
     copies = [
         pltpu.make_async_copy(source, target, sems.at[index])
         for index, (source, target) in enumerate(zip(sources, targets))
     ]
     for copy in copies:
         copy.start()
-    for copy in copies:
+    for copy in copies[:4]:
         copy.wait()
     dim, width = points_ref.shape
     rhs_rows = rhs_ref.shape[0]
@@ -184,9 +184,12 @@
     sub = lax.broadcasted_iota(jnp.int32, weight_ref.shape, 0)
     weight = jnp.where(sub == 0, own, jnp.where(sub == 1, first, second))
     weight_ref[...] = weight * THIRD
+    copies[4].wait()
     pick = lax.broadcasted_iota(jnp.int32, (width, skel), 0) == skel_ref[...]
     chosen = fold(raw(triple(scaled), jnp.where(pick, 1.0, 0.0).astype(BF16)))
+    copies[5].wait()
     coeff = times(rhs, pair(basis_ref[...]))
+    copies[6].wait()
     lifted = times(coeff, pair(lift_ref[0]))
     parts = [chosen, coeff, lifted]
     if rows > dim + 2 * rhs_rows:
@@ -292,7 +295,7 @@
 def half_kernel(*refs, groups):
     got_ref = refs[0]
     pick_refs = refs[1 : 1 + groups]
-    (mine_ref, near_ref, near_a_ref, near_b_ref, rhs_ref, noise_ref, basis_ref,
+    (mine_ref, near_ref, near_a_ref, rhs_ref, noise_ref, basis_ref,
      part_ref, left_ref, high_ref, low_ref, far_ref, base_ref, coeff_ref, gram_ref) = refs[1 + groups :]
     rhs_rows, skel = coeff_ref.shape
     dim = part_ref.shape[1] - rhs_rows
@@ -301,8 +304,7 @@
     far_ref[...] = far_part(got_ref, groups, left, high_ref, low_ref, dim, rhs_rows)
     for index, part in enumerate(picked(got_ref, pick_refs, 0, dim, rhs_rows)):
         part_ref[index] = part
-    near = near_ref[...] + near_a_ref[...] + near_b_ref[...]
-    base = (noise_ref[...] - SHIFT) * rhs_ref[...] + near
+    base = (noise_ref[...] - SHIFT) * rhs_ref[...] + (near_ref[...] + near_a_ref[...])
     base_ref[...] = base
     basis = basis_ref[...]
     both = pair(basis)
@@ -317,7 +319,7 @@
 def first_image_kernel(*refs, groups):
     got_ref = refs[0]
     pick_refs = refs[1 : 1 + groups]
-    (part_ref, left_ref, far_ref, base_ref, coeff_ref, gram_ref, rhs_ref, lift_ref, basis_ref,
+    (near_b_ref, part_ref, left_ref, far_ref, base_ref, coeff_ref, gram_ref, rhs_ref, lift_ref, basis_ref,
      shift_ref, send_ref, top_high_ref, top_low_ref, high_ref, low_ref) = refs[1 + groups :]
     rhs_rows, skel = coeff_ref.shape
     dim = part_ref.shape[1] - rhs_rows
@@ -332,10 +334,12 @@
     top = times_parts_t(jnp.concatenate([part[dim:] for part in parts], axis=1), high, low)
     lift = pair(lift_ref[0])
     row = (far + times_t(top, lift)) * THIRD
-    coeff = coeff_ref[...] + times(row, pair(gram_ref[...]))
+    near = near_b_ref[...]
+    basis = pair(basis_ref[...])
+    coeff = (coeff_ref[...] + times(near, basis)) + times(row, pair(gram_ref[...]))
     lifted = times(coeff, lift)
     rhs = rhs_ref[...]
-    shift = base_ref[...] + times_t(row, pair(basis_ref[...]))
+    shift = (base_ref[...] + near) + times_t(row, basis)
     shift_ref[...] = shift
     total = to_row(row_sum(rhs * rhs))
     along = to_row(row_sum(rhs * shift))
@@ -344,7 +348,7 @@
 
 
 def half_again_kernel(
-    got_ref, near_ref, near_a_ref, near_b_ref, shift_ref, noise_ref, high_ref, low_ref,
+    got_ref, near_ref, near_a_ref, shift_ref, noise_ref, high_ref, low_ref,
     part_ref, far_ref, base_ref,
 ):
     rhs_rows = far_ref.shape[0]
@@ -352,12 +356,11 @@
     far_ref[...] = far_again(got_ref, groups, high_ref, low_ref, rhs_rows)
     for index, part in enumerate(group_sums(got_ref, groups, rhs_rows)):
         part_ref[index] = part
-    near = near_ref[...] + near_a_ref[...] + near_b_ref[...]
-    base_ref[...] = noise_ref[...] * shift_ref[...] + near
+    base_ref[...] = noise_ref[...] * shift_ref[...] + (near_ref[...] + near_a_ref[...])
 
 
 def second_image_kernel(
-    got_ref, part_ref, far_ref, base_ref, high_ref, low_ref, top_high_ref, top_low_ref,
+    got_ref, near_b_ref, part_ref, far_ref, base_ref, high_ref, low_ref, top_high_ref, top_low_ref,
     rhs_ref, shift_ref, lift_ref, basis_ref, residual_ref, image_ref, alpha_ref, send_ref,
 ):
     rhs_rows, skel = far_ref.shape
@@ -377,7 +380,7 @@
     rhs = rhs_ref[...]
     row = (far + times_t(top, pair(lift_ref[0]))) * THIRD
     residual = keep * rhs - alpha * shift
-    second = base_ref[...] + times_t(row, pair(basis_ref[...]))
+    second = (base_ref[...] + near_b_ref[...]) + times_t(row, pair(basis_ref[...]))
     image = keep * (shift + SHIFT * rhs) - alpha * second
     residual_ref[...] = residual
     image_ref[...] = image
@@ -438,14 +441,14 @@
     rows = -(-(dim + 2 * rhs_rows) // 8) * 8
     rows_next = -(-(2 * rhs_rows + 2) // 8) * 8
     room = 8 + (2 * groups * half * rows * skel * 4 + 4 * half * skel * skel * 4) // MIB
-    inputs = [points, rhs, basis, transfer, noise, inv_scale, links, leaf_skel]
+    inputs = [points, rhs, basis, transfer, inv_scale, links, leaf_skel]
     scratch = [pltpu.VMEM(value.shape, value.dtype) for value in inputs]
-    for index in (5, 6):
+    for index in (4, 5):
         scratch[index] = pltpu.SMEM(inputs[index].shape, inputs[index].dtype)
     beside, send, weight = call(
         prepare_kernel,
         [((dim + rhs_rows, width), F32), ((groups * half, rows, skel), F32), ((8, skel), F32)],
-        inputs, space=pltpu.HBM, scratch=scratch + [pltpu.SemaphoreType.DMA((8,))],
+        inputs, space=pltpu.HBM, scratch=scratch + [pltpu.SemaphoreType.DMA((7,))],
         limit=60,
     )
     got = spread(send, members)
@@ -473,14 +476,14 @@
         functools.partial(half_kernel, groups=groups),
         [((groups, dim + rhs_rows, skel), F32), ((skel, skel), BF16), far_shape, far_shape,
          (small, F32), (wide, F32), (small, F32), ((skel, skel), F32)],
-        [got, *picks, send, near, near_a, near_b, rhs, noise, basis],
+        [got, *picks, send, near, near_a, rhs, noise, basis],
         limit=room, flops=10**9,
     )
     shift, send, top_high, top_low, peer_high, peer_low = call(
         functools.partial(first_image_kernel, groups=groups),
         [(wide, F32), ((groups * half, rows_next, skel), F32), top_shape, top_shape,
          far_shape, far_shape],
-        [peer, *picks, part, left, far, base, coeff, gram, rhs, transfer, basis],
+        [peer, *picks, near_b, part, left, far, base, coeff, gram, rhs, transfer, basis],
         limit=room,
     )
     got = spread(send, members)
@@ -493,13 +496,14 @@
     part, far, base = call(
         half_again_kernel,
         [((groups, rows_next - rhs_rows, skel), F32), (small, F32), (wide, F32)],
-        [got, near, near_a, near_b, shift, noise, high, low],
+        [got, near, near_a, shift, noise, high, low],
         limit=room, flops=10**9,
     )
     residual, image, alpha, send = call(
         second_image_kernel,
         [(wide, F32), (wide, F32), (small, F32), ((boxes * groups, 1, skel), F32)],
-        [peer, part, far, base, peer_high, peer_low, top_high, top_low, rhs, shift, transfer, basis],
+        [peer, near_b, part, far, base, peer_high, peer_low, top_high, top_low,
+         rhs, shift, transfer, basis],
         limit=room,
     )
     got = spread(send)

time: 64 us -> 61.6 us (0.963)
  starting transfers between devices: 19.3 us -> 16.7 us
  waiting for transfers between devices: 9.9 us -> 12.5 us
  blocking collectives: 12.1 us -> 9.76 us
    ppermute x7, starting transfers between devices: 10.6 us -> 5.21 us  [pass_on(): return lax.ppermute(value, axis, pairs)]
    all_to_all x2, starting transfers between devices: 8.66 us -> 11.4 us  [spread(): lax.all_to_all(value, ('grp', 'leaf'), 0, 0, tiled=True, axis_index_group...]
    all_to_all x2, waiting for transfers between devices: 9.88 us -> 12.5 us  [spread(): lax.all_to_all(value, ('grp', 'leaf'), 0, 0, tiled=True, axis_index_group...]
    all_to_all x1, blocking collectives: 12.1 us -> 9.76 us  [spread(): lax.all_to_all(value, ('grp', 'leaf'), 0, 0, tiled=True, axis_index_group...]
  transfers between devices with their start and end apart: 9 -> 9, of which waited for: 2 -> 2; matrix products, arithmetic and copies ran while one was open for 0% -> 0% of each run, Pallas kernels for 24% -> 25%
where the time goes in v2:
time: 61.6 us; the launch traced here: 61.3 us
  Pallas kernels  21.5 us (35%)
  starting transfers between devices  16.7 us (27%)
  waiting for transfers between devices  12.5 us (20%)
  blocking collectives  9.76 us (16%)
  between operations  0.82 us (1%)
    pallas_call x12, Pallas kernels, call(): pl.pallas_call(kernel, out_shape=[jax.ShapeDtypeStruct(s, d) for s, d in...  21.5 us
    all_to_all x2, waiting for transfers between devices, spread(): lax.all_to_all(value, ('grp', 'leaf'), 0, 0, tiled=True, axis_index_group...  12.5 us
    all_to_all x2, starting transfers between devices, spread(): lax.all_to_all(value, ('grp', 'leaf'), 0, 0, tiled=True, axis_index_group...  11.4 us
    all_to_all x1, blocking collectives, spread(): lax.all_to_all(value, ('grp', 'leaf'), 0, 0, tiled=True, axis_index_group...  9.76 us
    ppermute x7, starting transfers between devices, pass_on(): return lax.ppermute(value, axis, pairs)  5.21 us
  transfers between devices with their start and end apart: 9, of which 2 were waited for; matrix products, arithmetic and copies ran while one was open for 0% of the time, Pallas kernels for 25%

profile of v2, /device:TPU:0, one launch (start us, length us, event | category | flops | bytes accessed | tf_op | source)
XLA Modules:
  0.0 61.3 jit_solution(9147361684135475368)
XLA Ops:
  0.6 2.3 %shard_map.104 = (f32[24,1024]{1,0:T(8,128)}, f32[16,40,128]{2,1,0:T(8,128)}, f32[8,128]{1,0:T(8,128)}) custom-call(f32[8,1024]{1,0:T(8,128)} %points_hbm.1, f32[16,1024]{1,0:T(8,128)} %rhs_ref.3, f32[1024,128]{1,0:T(8,128)} %basis_ref.1, f32[1,128,128]{2,1,0:T(8,128)} %lift_ref.1, f32[8]{0:T(128)} %scale_hbm.1, s32[1,2]{1,0:T(1,128)} %links_hbm.1, ...), custom_call_target="tpu_custom_call" | custom-call | flops 1000000 | bytes 1048576 | tf_op jit(solution)/shard_map/pallas_call | solution.py:142
  2.9 0.0 copy-start.4
  2.9 0.6 collective-permute-start.3
  3.5 0.7 %collective-permute-start.2 = (f32[24,1024]{1,0:T(8,128)}, f32[24,1024]{1,0:T(8,128)S(1)}, u32[]{:S(2)}, u32[]{:S(2)}) collective-permute-start(f32[24,1024]{1,0:T(8,128)} %get-tuple-element.28.own_ref.other_ref.vec_ref), channel_id=1, source_target_pairs={{1,2},{2,1},{3,4},{4,3},{5,6},{6,5},{7,8},{8,7},{9,10},{10,9},{11,... | collective-permute-start | bytes 294920 | tf_op jit(solution)/shard_map/ppermute | solution.py:420
  4.2 0.0 copy-done.4
  4.2 2.6 %collective-permute-start.1 = (s32[1,128]{1,0:T(1,128)S(1)}, s32[1,128]{1,0:T(1,128)S(1)}, u32[]{:S(2)}, u32[]{:S(2)}) collective-permute-start(s32[1,128]{1,0:T(1,128)S(1)} %copy-done.4), channel_id=1, source_target_pairs={{0,16},{16,0},{1,17},{17,1},{2,18},{18,2},{3,19},{19,3},{4,20},{20... | collective-permute-start | bytes 1544 | tf_op jit(solution)/shard_map/ppermute | solution.py:420
  6.7 0.0 copy-start.5
  6.7 0.0 copy-start.7
  6.7 7.9 %all-to-all-start = ((f32[16,40,128]{2,1,0:T(8,128)}), f32[16,40,128]{2,1,0:T(8,128)S(1)}, u32[]{:S(2)}, u32[]{:S(2)}) async-start(f32[16,40,128]{2,1,0:T(8,128)} %get-tuple-element.26.refs_3_), calls=%async_computation | async-start | bytes 655360 | tf_op jit(solution)/shard_map/all_to_all | solution.py:414
  14.7 0.0 copy-done.5
  14.7 0.0 copy-done.7
  14.7 2.3 %shard_map.106.refs_4_ = f32[16,1024]{1,0:T(8,128)S(1)} custom-call(f32[8,128]{1,0:T(8,128)S(1)} %copy-done.7, f32[24,1024]{1,0:T(8,128)S(1)} %copy-done.5, f32[24,1024]{1,0:T(8,128)S(1)} %copy-done.5, f32[24,1024]{1,0:T(8,128)S(1)} %copy-done.5), custom_call_target="tpu_custom_call" | custom-call | flops 4000000000 | bytes 1048576 | tf_op jit(solution)/shard_map/pallas_call | solution.py:142
  17.0 0.0 collective-permute-done.3.other_ref.vec_ref
  17.0 2.3 %shard_map.107.refs_5_ = f32[16,1024]{1,0:T(8,128)S(1)} custom-call(f32[8,128]{1,0:T(8,128)S(1)} %copy-done.7, f32[24,1024]{1,0:T(8,128)S(1)} %copy-done.5, f32[24,1024]{1,0:T(8,128)S(1)} %collective-permute-done.3.other_ref.vec_ref, f32[24,1024]{1,0:T(8,128)S(1)} %collective-permute-done.3.other_ref.vec_ref), custom_call_target="tpu_custom_call" | custom-call | flops 4000000000 | bytes 1048576 | tf_op jit(solution)/shard_map/pallas_call | solution.py:142
  19.3 0.0 copy-start
  19.3 0.0 copy-start.1
  19.3 0.0 copy-start.3
  19.3 0.0 copy-start.6
  19.3 6.6 %all-to-all-done.refs_0_ = f32[16,40,128]{2,1,0:T(8,128)S(1)} async-done(((f32[16,40,128]{2,1,0:T(8,128)}), f32[16,40,128]{2,1,0:T(8,128)S(1)}, u32[]{:S(2)}, u32[]{:S(2)}) %all-to-all-start) | async-done | bytes 327712 | tf_op jit(solution)/shard_map/all_to_all | solution.py:414
  26.0 0.0 collective-permute-start
  26.0 0.0 collective-permute-done.2.other_ref.vec_ref
  26.0 2.3 %shard_map.105.refs_3_ = f32[16,1024]{1,0:T(8,128)S(1)} custom-call(f32[8,128]{1,0:T(8,128)S(1)} %copy-done.7, f32[24,1024]{1,0:T(8,128)S(1)} %copy-done.5, f32[24,1024]{1,0:T(8,128)S(1)} %collective-permute-done.2.other_ref.vec_ref, f32[24,1024]{1,0:T(8,128)S(1)} %collective-permute-done.2.other_ref.vec_ref), custom_call_target="tpu_custom_call" | custom-call | flops 4000000000 | bytes 1048576 | tf_op jit(solution)/shard_map/pallas_call | solution.py:142
  28.2 0.0 collective-permute-done.1.refs_2_
  28.2 0.0 copy-done
  28.3 0.0 copy-done.1
  28.3 0.0 copy-done.3
  28.3 0.0 copy-done.6
  28.3 0.0 copy-start.2
  28.3 1.1 %shard_map.108 = (f32[2,24,128]{2,1,0:T(8,128)S(1)}, bf16[128,128]{1,0:T(8,128)(2,1)S(1)}, bf16[1,128,1024]{2,1,0:T(8,128)(2,1)S(1)}, bf16[1,128,1024]{2,1,0:T(8...) custom-call(f32[16,40,128]{2,1,0:T(8,128)S(1)} %all-to-all-done.refs, ...), custom_call_target="tpu_custom_call" | custom-call | flops 1000000000 | bytes 1048576 | tf_op jit(solution)/shard_map/pallas_call | solution.py:142
  29.4 0.0 collective-permute-done.refs_0_
  29.4 0.0 copy-done.2
  29.4 2.2 %shard_map.109 = (f32[16,1024]{1,0:T(8,128)S(1)}, f32[16,40,128]{2,1,0:T(8,128)}, bf16[128,256]{1,0:T(8,128)(2,1)S(1)}, bf16[128,256]{1,0:T(8,128)(2,1)S(1)}, bf...) custom-call(f32[16,40,128]{2,1,0:T(8,128)S(1)} %collective-permute-done.refs_0_, ...), custom_call_target="tpu_custom_call" | custom-call | flops 1000000 | bytes 1048576 | tf_op jit(solution)/shard_map/pallas_call | solution.py:142
  31.6 3.5 %all-to-all-start.1 = ((f32[16,40,128]{2,1,0:T(8,128)}), f32[16,40,128]{2,1,0:T(8,128)S(1)}, u32[]{:S(2)}, u32[]{:S(2)}) async-start(f32[16,40,128]{2,1,0:T(8,128)} %get-tuple-element.35), calls=%async_computation.1 | async-start | bytes 655360 | tf_op jit(solution)/shard_map/all_to_all | solution.py:414
  35.1 0.6 collective-permute-start.6
  35.7 2.3 %shard_map.111.near_ref = f32[16,1024]{1,0:T(8,128)S(1)} custom-call(f32[8,128]{1,0:T(8,128)S(1)} %copy-done.7, f32[24,1024]{1,0:T(8,128)S(1)} %copy-done.5, f32[24,1024]{1,0:T(8,128)S(1)} %copy-done.5, f32[16,1024]{1,0:T(8,128)S(1)} %get-tuple-element.36.vec_ref.shift_ref), custom_call_target="tpu_custom_call" | custom-call | flops 4000000000 | bytes 1048576 | tf_op jit(solution)/shard_map/pallas_call | solution.py:142
  38.0 0.9 %collective-permute-start.5 = (f32[16,1024]{1,0:T(8,128)S(1)}, f32[16,1024]{1,0:T(8,128)S(1)}, u32[]{:S(2)}, u32[]{:S(2)}) collective-permute-start(f32[16,1024]{1,0:T(8,128)S(1)} %get-tuple-element.36.vec_ref.shift_ref), channel_id=1, source_target_pairs={{1,2},{2,1},{3,4},{4,3},{5,6},{6,5},{7,8},{8,7},{9,10},{10,9},{11,... | collective-permute-start | bytes 196616 | tf_op jit(solution)/shard_map/ppermute | solution.py:420
  38.8 0.0 collective-permute-done.6.vec_ref
  38.9 2.3 %shard_map.112.near_a_ref = f32[16,1024]{1,0:T(8,128)S(1)} custom-call(f32[8,128]{1,0:T(8,128)S(1)} %copy-done.7, f32[24,1024]{1,0:T(8,128)S(1)} %copy-done.5, f32[24,1024]{1,0:T(8,128)S(1)} %collective-permute-done.3.other_ref.vec_ref, f32[16,1024]{1,0:T(8,128)S(1)} %collective-permute-done.6.vec_ref), custom_call_target="tpu_custom_call" | custom-call | flops 4000000000 | bytes 1048576 | tf_op jit(solution)/shard_map/pallas_call | solution.py:142
  41.1 5.8 %all-to-all-done.1.got_ref = f32[16,40,128]{2,1,0:T(8,128)S(1)} async-done(((f32[16,40,128]{2,1,0:T(8,128)}), f32[16,40,128]{2,1,0:T(8,128)S(1)}, u32[]{:S(2)}, u32[]{:S(2)}) %all-to-all-start.1) | async-done | bytes 327712 | tf_op jit(solution)/shard_map/all_to_all | solution.py:414
  47.0 0.0 collective-permute-start.4
  47.0 0.0 collective-permute-done.5.vec_ref
  47.0 2.3 %shard_map.110.near_b_ref = f32[16,1024]{1,0:T(8,128)S(1)} custom-call(f32[8,128]{1,0:T(8,128)S(1)} %copy-done.7, f32[24,1024]{1,0:T(8,128)S(1)} %copy-done.5, f32[24,1024]{1,0:T(8,128)S(1)} %collective-permute-done.2.other_ref.vec_ref, f32[16,1024]{1,0:T(8,128)S(1)} %collective-permute-done.5.vec_ref), custom_call_target="tpu_custom_call" | custom-call | flops 4000000000 | bytes 1048576 | tf_op jit(solution)/shard_map/pallas_call | solution.py:142
  49.2 0.3 shard_map.113
  49.5 0.0 collective-permute-done.4.got_ref
  49.5 1.1 %shard_map.114 = (f32[16,1024]{1,0:T(8,128)S(1)}, f32[16,1024]{1,0:T(8,128)S(1)}, f32[16,128]{1,0:T(8,128)S(1)}, f32[32,1,128]{2,1,0:T(1,128)S(1)}) custom-call(f32[16,40,128]{2,1,0:T(8,128)S(1)} %collective-permute-done.4.got_ref, f32[16,1024]{1,0:T(8,128)S(1)} %shard_map.110.near_b_ref, f32[2,24,128]{2,1,0:T(8,128)S(1)} %get-tuple-element.39.part_ref, ...), custom_call_target="tpu_custom_call" | custom-call | flops 1000000 | bytes 1048576 | tf_op jit(solution)/shard_map/pallas_call | solution.py:142
  50.6 9.8 %all_to_all.15.got_ref = f32[32,1,128]{2,1,0:T(1,128)S(1)} all-to-all(f32[32,1,128]{2,1,0:T(1,128)S(1)} %get-tuple-element.46), channel_id=1, replica_groups=mesh['grp'=2,'leaf'=16] {'grp','leaf'}, dimensions={0} | all-to-all | bytes 32768 | tf_op jit(solution)/shard_map/all_to_all | solution.py:414
  60.4 0.9 %shard_map.115 = (f32[16,1024]{1,0:T(8,128)}, f32[16,1024]{1,0:T(8,128)}) custom-call(f32[32,1,128]{2,1,0:T(1,128)S(1)} %all_to_all.15.got_ref, f32[16,128]{1,0:T(8,128)S(1)} %get-tuple-element.47.alpha_ref, f32[16,1024]{1,0:T(8,128)S(1)} %copy-done.1, f32[16,1024]{1,0:T(8,128)S(1)} %get-tuple-element.36.vec_ref.shift_ref, ...), custom_call_target="tpu_custom_call" | custom-call | flops 1000000 | bytes 1048576 | tf_op jit(solution)/shard_map/pallas_call | solution.py:142
Async XLA Ops:
  2.9 1.2 %copy-start.4 = (s32[1,128]{1,0:T(1,128)S(1)}, s32[1,128]{1,0:T(1,128)}, u32[]{:S(2)}) copy-start(s32[1,128]{1,0:T(1,128)} %refs_1_.3) | copy-start | bytes 1540
  2.9 14.0 %collective-permute-start.3 = (f32[24,1024]{1,0:T(8,128)}, f32[24,1024]{1,0:T(8,128)S(1)}, u32[]{:S(2)}, u32[]{:S(2)}) collective-permute-start(f32[24,1024]{1,0:T(8,128)} %get-tuple-element.28.own_ref.other_ref.vec_ref), channel_id=1, source_target_pairs={{0,1},{1,0},{2,3},{3,2},{4,5},{5,4},{6,7},{7,6},{8,9},{9,8},{10,11... | collective-permute-start | bytes 294920 | tf_op jit(solution)/shard_map/ppermute | solution.py:420
  3.5 22.4 %collective-permute-start.2 = (f32[24,1024]{1,0:T(8,128)}, f32[24,1024]{1,0:T(8,128)S(1)}, u32[]{:S(2)}, u32[]{:S(2)}) collective-permute-start(f32[24,1024]{1,0:T(8,128)} %get-tuple-element.28.own_ref.other_ref.vec_ref), channel_id=1, source_target_pairs={{1,2},{2,1},{3,4},{4,3},{5,6},{6,5},{7,8},{8,7},{9,10},{10,9},{11,... | collective-permute-start | bytes 294920 | tf_op jit(solution)/shard_map/ppermute | solution.py:420
  4.2 24.1 %collective-permute-start.1 = (s32[1,128]{1,0:T(1,128)S(1)}, s32[1,128]{1,0:T(1,128)S(1)}, u32[]{:S(2)}, u32[]{:S(2)}) collective-permute-start(s32[1,128]{1,0:T(1,128)S(1)} %copy-done.4), channel_id=1, source_target_pairs={{0,16},{16,0},{1,17},{17,1},{2,18},{18,2},{3,19},{19,3},{4,20},{20... | collective-permute-start | bytes 1544 | tf_op jit(solution)/shard_map/ppermute | solution.py:420
  6.7 7.9 %copy-start.5 = (f32[24,1024]{1,0:T(8,128)S(1)}, f32[24,1024]{1,0:T(8,128)}, u32[]{:S(2)}) copy-start(f32[24,1024]{1,0:T(8,128)} %get-tuple-element.28.own_ref.other_ref.vec_ref) | copy-start | bytes 294916
  6.7 7.9 %copy-start.7 = (f32[8,128]{1,0:T(8,128)S(1)}, f32[8,128]{1,0:T(8,128)}, u32[]{:S(2)}) copy-start(f32[8,128]{1,0:T(8,128)} %get-tuple-element.27.weight_ref) | copy-start | bytes 12292
  6.7 19.2 %all-to-all-start = ((f32[16,40,128]{2,1,0:T(8,128)}), f32[16,40,128]{2,1,0:T(8,128)S(1)}, u32[]{:S(2)}, u32[]{:S(2)}) async-start(f32[16,40,128]{2,1,0:T(8,128)} %get-tuple-element.26.refs_3_), calls=%async_computation | async-start | bytes 655360 | tf_op jit(solution)/shard_map/all_to_all | solution.py:414
  19.3 9.0 %copy-start = (f32[1024,128]{1,0:T(8,128)S(1)}, f32[1024,128]{1,0:T(8,128)}, u32[]{:S(2)}) copy-start(f32[1024,128]{1,0:T(8,128)} %basis_ref.1) | copy-start | bytes 1572868
  19.3 9.0 %copy-start.1 = (f32[16,1024]{1,0:T(8,128)S(1)}, f32[16,1024]{1,0:T(8,128)}, u32[]{:S(2)}) copy-start(f32[16,1024]{1,0:T(8,128)} %rhs_ref.3) | copy-start | bytes 196612
  19.3 9.0 %copy-start.3 = (f32[16,40,128]{2,1,0:T(8,128)S(1)}, f32[16,40,128]{2,1,0:T(8,128)}, u32[]{:S(2)}) copy-start(f32[16,40,128]{2,1,0:T(8,128)} %get-tuple-element.26.refs_3_) | copy-start | bytes 983044
  19.3 9.0 %copy-start.6 = (f32[1024]{0:T(1024)S(1)}, f32[1024]{0:T(1024)}, u32[]{:S(2)}) copy-start(f32[1024]{0:T(1024)} %param.13) | copy-start | bytes 12292
  26.0 3.4 %collective-permute-start = (f32[16,40,128]{2,1,0:T(8,128)S(1)}, f32[16,40,128]{2,1,0:T(8,128)S(1)}, u32[]{:S(2)}, u32[]{:S(2)}) collective-permute-start(f32[16,40,128]{2,1,0:T(8,128)S(1)} %all-to-all-done.refs_0_), channel_id=1, source_target_pairs={{0,1},{1,0},{2,3},{3,2},{4,5},{5,4},{6,7},{7,6},{8,9},{9,8},{10,11... | collective-permute-start | bytes 983048 | tf_op jit(solution)/shard_map/ppermute | solution.py:420
  28.3 1.1 %copy-start.2 = (f32[1,128,128]{2,1,0:T(8,128)S(1)}, f32[1,128,128]{2,1,0:T(8,128)}, u32[]{:S(2)}) copy-start(f32[1,128,128]{2,1,0:T(8,128)} %lift_ref.1) | copy-start | bytes 196612
  31.6 15.4 %all-to-all-start.1 = ((f32[16,40,128]{2,1,0:T(8,128)}), f32[16,40,128]{2,1,0:T(8,128)S(1)}, u32[]{:S(2)}, u32[]{:S(2)}) async-start(f32[16,40,128]{2,1,0:T(8,128)} %get-tuple-element.35), calls=%async_computation.1 | async-start | bytes 655360 | tf_op jit(solution)/shard_map/all_to_all | solution.py:414
  35.1 3.7 %collective-permute-start.6 = (f32[16,1024]{1,0:T(8,128)S(1)}, f32[16,1024]{1,0:T(8,128)S(1)}, u32[]{:S(2)}, u32[]{:S(2)}) collective-permute-start(f32[16,1024]{1,0:T(8,128)S(1)} %get-tuple-element.36.vec_ref.shift_ref), channel_id=1, source_target_pairs={{0,1},{1,0},{2,3},{3,2},{4,5},{5,4},{6,7},{7,6},{8,9},{9,8},{10,11... | collective-permute-start | bytes 196616 | tf_op jit(solution)/shard_map/ppermute | solution.py:420
  38.0 9.0 %collective-permute-start.5 = (f32[16,1024]{1,0:T(8,128)S(1)}, f32[16,1024]{1,0:T(8,128)S(1)}, u32[]{:S(2)}, u32[]{:S(2)}) collective-permute-start(f32[16,1024]{1,0:T(8,128)S(1)} %get-tuple-element.36.vec_ref.shift_ref), channel_id=1, source_target_pairs={{1,2},{2,1},{3,4},{4,3},{5,6},{6,5},{7,8},{8,7},{9,10},{10,9},{11,... | collective-permute-start | bytes 196616 | tf_op jit(solution)/shard_map/ppermute | solution.py:420
  47.0 2.6 %collective-permute-start.4 = (f32[16,40,128]{2,1,0:T(8,128)S(1)}, f32[16,40,128]{2,1,0:T(8,128)S(1)}, u32[]{:S(2)}, u32[]{:S(2)}) collective-permute-start(f32[16,40,128]{2,1,0:T(8,128)S(1)} %all-to-all-done.1.got_ref), channel_id=1, source_target_pairs={{0,1},{1,0},{2,3},{3,2},{4,5},{5,4},{6,7},{7,6},{8,9},{9,8},{10,11... | collective-permute-start | bytes 983048 | tf_op jit(solution)/shard_map/ppermute | solution.py:420

commit v3 on v2

--- a/solution.py
+++ b/solution.py
@@ -12,8 +12,7 @@
 F32 = jnp.float32
 BF16 = jnp.bfloat16
 LOG2E = math.log2(math.e)
-UNIT = math.sqrt(5.0)
-THIRD = 1.0 / 3.0
+UNIT = math.sqrt(5.0) / 3.0
 MIB = 1 << 20
 SHIFT = 3.0
 
@@ -98,11 +97,10 @@
     return jnp.concatenate(rows, axis=0).astype(BF16)
 
 
-def matern3(square):
+def matern(square):
     square = jnp.maximum(square, 1e-30)
     root = square * lax.rsqrt(square)
-    base = root + 1.5
-    return (base * base + 0.75) * jnp.exp2(root * (-LOG2E))
+    return ((square + root) + 1.0 / 3.0) * jnp.exp2(root * (-3.0 * LOG2E))
 
 
 def to_row(column):
@@ -130,12 +128,12 @@
     return lax.fori_loop(0, count, body, init)
 
 
-def fill(ref, block):
+def fill(ref, block, first=0, count=None):
     def put(index, carry):
-        ref[index] = block
+        ref[first + index] = block
         return carry
 
-    each(ref.shape[0], put, 0)
+    each(ref.shape[0] if count is None else count, put, 0)
 
 
 def call(kernel, outs, ins, space=pltpu.VMEM, scratch=(), limit=8, flops=1_000_000):
@@ -151,12 +149,13 @@
 
 
 def prepare_kernel(
-    points_hbm, rhs_hbm, basis_hbm, lift_hbm, scale_hbm, links_hbm, skel_hbm,
-    beside_ref, send_ref, weight_ref,
-    points_ref, rhs_ref, basis_ref, lift_ref, scale_ref, links_ref, skel_ref, sems,
+    points_hbm, rhs_hbm, basis_hbm, lift_hbm, scale_hbm, links_hbm, skel_hbm, pick_hbm,
+    beside_ref, send_ref, weight_ref, mine_ref,
+    points_ref, rhs_ref, basis_ref, lift_ref, scale_ref, links_ref, skel_ref, pick_ref, sems,
+    *, groups,
 ):
-    sources = (points_hbm, scale_hbm, links_hbm, rhs_hbm, skel_hbm, basis_hbm, lift_hbm)
-    targets = (points_ref, scale_ref, links_ref, rhs_ref, skel_ref, basis_ref, lift_ref)
+    sources = (points_hbm, scale_hbm, links_hbm, rhs_hbm, skel_hbm, basis_hbm, lift_hbm, pick_hbm)
+    targets = (points_ref, scale_ref, links_ref, rhs_ref, skel_ref, basis_ref, lift_ref, pick_ref)
     copies = [
         pltpu.make_async_copy(source, target, sems.at[index])
         for index, (source, target) in enumerate(zip(sources, targets))
@@ -183,7 +182,7 @@
     second = odd * upper + (1.0 - odd) * lower
     sub = lax.broadcasted_iota(jnp.int32, weight_ref.shape, 0)
     weight = jnp.where(sub == 0, own, jnp.where(sub == 1, first, second))
-    weight_ref[...] = weight * THIRD
+    weight_ref[...] = weight * 3.0
     copies[4].wait()
     pick = lax.broadcasted_iota(jnp.int32, (width, skel), 0) == skel_ref[...]
     chosen = fold(raw(triple(scaled), jnp.where(pick, 1.0, 0.0).astype(BF16)))
@@ -191,10 +190,45 @@
     coeff = times(rhs, pair(basis_ref[...]))
     copies[6].wait()
     lifted = times(coeff, pair(lift_ref[0]))
-    parts = [chosen, coeff, lifted]
+    copies[7].wait()
+    index = jnp.concatenate([pick_ref[...].astype(F32), jnp.zeros((rhs_rows - 1, skel), F32)], axis=0)
+    mine_ref[...] = jnp.concatenate([chosen, coeff, index], axis=0)
+    rest = [lifted]
     if rows > dim + 2 * rhs_rows:
-        parts.append(jnp.zeros((rows - dim - 2 * rhs_rows, skel), F32))
-    fill(send_ref, jnp.concatenate(parts, axis=0))
+        rest.append(jnp.zeros((rows - dim - 2 * rhs_rows, skel), F32))
+    half = send_ref.shape[0] // groups
+    for shift in range(groups):
+        first = lax.rem(lax.axis_index("grp") + shift, groups) * half
+        middle = index if shift else coeff
+        fill(send_ref, jnp.concatenate([chosen, middle, *rest], axis=0), first, half)
+
+
+def self_kernel(weight_ref, own_ref, vec_ref, out_ref, high_ref, low_ref):
+    rhs_rows, width = out_ref.shape
+    dim = own_ref.shape[0] - rhs_rows
+    start = vec_ref.shape[0] - rhs_rows
+    block = min(256, width)
+    left = stack_left(own_ref[0:dim, :])
+    right = stack_right(own_ref[0:dim, :])
+    vec = triple(vec_ref[start:, :])
+    weight = weight_ref[0:1, 0:1]
+    count = width // block
+    for c in range(count):
+        cols = slice(c * block, (c + 1) * block)
+        for i in range(c + 1):
+            rows = slice(i * block, (i + 1) * block)
+            high, low = split2(matern(raw(left[rows], right[:, cols])))
+            high_ref[rows, cols] = high
+            low_ref[rows, cols] = low
+    for c in range(count):
+        cols = slice(c * block, (c + 1) * block)
+        above = slice(0, (c + 1) * block)
+        total = raw(vec[:, above], high_ref[above, cols]) + raw(vec[:, above], low_ref[above, cols])
+        if c + 1 < count:
+            rest = slice((c + 1) * block, width)
+            total = total + raw_t(vec[:, rest], high_ref[cols, rest])
+            total = total + raw_t(vec[:, rest], low_ref[cols, rest])
+        out_ref[:, cols] = fold(total) * weight
 
 
 def near_kernel(weight_ref, own_ref, other_ref, vec_ref, out_ref, *, kind):
@@ -211,7 +245,7 @@
         total = jnp.zeros((3 * rhs_rows, block), F32)
         for i in range(width // block):
             rows = slice(i * block, (i + 1) * block)
-            high, low = split2(matern3(raw(left[rows], right[:, cols])))
+            high, low = split2(matern(raw(left[rows], right[:, cols])))
             total = total + raw(vec[:, rows], high) + raw(vec[:, rows], low)
         out_ref[:, cols] = fold(total) * weight
 
@@ -223,20 +257,24 @@
     return step, boxes // step
 
 
-def picked(ref, pick_refs, swapped, dim, rhs_rows):
+def picked(ref, mine_ref, groups, swapped, dim, rhs_rows):
     skel = ref.shape[2]
-    groups = len(pick_refs)
     half = ref.shape[0] // groups
     parity = lax.rem(lax.axis_index("leaf") + swapped, 2)
     out = []
-    for shift, pick_ref in enumerate(pick_refs):
+    for shift in range(groups):
         first = lax.rem(lax.axis_index("grp") + groups - shift, groups) * half
-
-        def body(index, carry, first=first, pick_ref=pick_ref):
+        if shift:
+            wanted = ref[first, dim : dim + 1, :]
+        else:
+            wanted = mine_ref[dim + rhs_rows : dim + rhs_rows + 1, :]
+        wanted = wanted.astype(jnp.int32)
+
+        def body(index, carry, first=first, wanted=wanted):
             chosen, summed = carry
             block = ref[first + index]
             place = lax.broadcasted_iota(jnp.int32, (skel, skel), 0)
-            pick = place + (2 * index + parity) * skel == pick_ref[...]
+            pick = place + (2 * index + parity) * skel == wanted
             pick = jnp.where(pick, 1.0, 0.0).astype(BF16)
             chosen = chosen + raw(triple(block[0:dim]), pick)
             return chosen, summed + block[dim + rhs_rows : dim + 2 * rhs_rows]
@@ -257,7 +295,7 @@
         blocks = [ref[first + index * step + j] for j in range(step)]
         right = stack_right(jnp.concatenate([block[0:dim] for block in blocks], axis=1))
         coeff = jnp.concatenate([block[dim : dim + rhs_rows] for block in blocks], axis=1)
-        high, low = split2(matern3(raw(left, right)))
+        high, low = split2(matern(raw(left, right)))
         high_ref[index] = high
         low_ref[index] = low
         return total + times_parts_t(coeff, high, low)
@@ -292,59 +330,62 @@
     return out
 
 
-def half_kernel(*refs, groups):
-    got_ref = refs[0]
-    pick_refs = refs[1 : 1 + groups]
-    (mine_ref, near_ref, near_a_ref, rhs_ref, noise_ref, basis_ref,
-     part_ref, left_ref, high_ref, low_ref, far_ref, base_ref, coeff_ref, gram_ref) = refs[1 + groups :]
-    rhs_rows, skel = coeff_ref.shape
-    dim = part_ref.shape[1] - rhs_rows
-    left = stack_left(mine_ref[0, 0:dim, :])
-    left_ref[...] = left
-    far_ref[...] = far_part(got_ref, groups, left, high_ref, low_ref, dim, rhs_rows)
-    for index, part in enumerate(picked(got_ref, pick_refs, 0, dim, rhs_rows)):
-        part_ref[index] = part
+def base_kernel(
+    mine_ref, near_ref, near_a_ref, rhs_ref, noise_ref, basis_ref,
+    base_ref, coeff_ref, gram_ref, copy_ref,
+):
+    skel = basis_ref.shape[1]
+    copy_ref[...] = mine_ref[...]
     base = (noise_ref[...] - SHIFT) * rhs_ref[...] + (near_ref[...] + near_a_ref[...])
     base_ref[...] = base
     basis = basis_ref[...]
     both = pair(basis)
     coeff_ref[...] = times(base, both)
-    flat = basis.T
-    square = raw(jnp.concatenate(split2(flat), axis=0), both)
+    square = raw(jnp.concatenate(split2(basis.T), axis=0), both)
     gram_ref[...] = (
         square[:skel, :skel] + square[:skel, skel:] + (square[skel:, :skel] + square[skel:, skel:])
     )
 
 
+def half_kernel(
+    got_ref, mine_ref, part_ref, left_ref, high_ref, low_ref, far_ref, *, groups
+):
+    rhs_rows = far_ref.shape[0]
+    dim = part_ref.shape[1] - rhs_rows
+    left = stack_left(mine_ref[0:dim, :])
+    left_ref[...] = left
+    far_ref[...] = far_part(got_ref, groups, left, high_ref, low_ref, dim, rhs_rows)
+    for index, part in enumerate(picked(got_ref, mine_ref, groups, 0, dim, rhs_rows)):
+        part_ref[index] = part
+
+
 def first_image_kernel(*refs, groups):
-    got_ref = refs[0]
-    pick_refs = refs[1 : 1 + groups]
-    (near_b_ref, part_ref, left_ref, far_ref, base_ref, coeff_ref, gram_ref, rhs_ref, lift_ref, basis_ref,
-     shift_ref, send_ref, top_high_ref, top_low_ref, high_ref, low_ref) = refs[1 + groups :]
+    (got_ref, near_b_ref, part_ref, left_ref, far_ref, base_ref, coeff_ref, gram_ref, mine_ref, rhs_ref, lift_ref, basis_ref,
+     shift_ref, send_ref, top_high_ref, top_low_ref, high_ref, low_ref) = refs
     rhs_rows, skel = coeff_ref.shape
     dim = part_ref.shape[1] - rhs_rows
-    parts = picked(got_ref, pick_refs, 1, dim, rhs_rows)
+    parts = picked(got_ref, mine_ref, groups, 1, dim, rhs_rows)
     parts = [part + part_ref[index] for index, part in enumerate(parts)]
     far = far_ref[...] + far_part(got_ref, groups, left_ref[...], high_ref, low_ref, dim, rhs_rows)
     left = stack_left(parts[0][0:dim])
     right = stack_right(jnp.concatenate([part[0:dim] for part in parts], axis=1))
-    high, low = split2(matern3(raw(left, right)))
+    high, low = split2(matern(raw(left, right)))
     top_high_ref[...] = high
     top_low_ref[...] = low
     top = times_parts_t(jnp.concatenate([part[dim:] for part in parts], axis=1), high, low)
     lift = pair(lift_ref[0])
-    row = (far + times_t(top, lift)) * THIRD
+    row = (far + times_t(top, lift)) * 3.0
     near = near_b_ref[...]
     basis = pair(basis_ref[...])
     coeff = (coeff_ref[...] + times(near, basis)) + times(row, pair(gram_ref[...]))
     lifted = times(coeff, lift)
     rhs = rhs_ref[...]
-    shift = (base_ref[...] + near) + times_t(row, basis)
-    shift_ref[...] = shift
+    base = base_ref[...] + near
     total = to_row(row_sum(rhs * rhs))
-    along = to_row(row_sum(rhs * shift))
+    along = to_row(row_sum(rhs * base) + row_sum(mine_ref[dim : dim + rhs_rows, :] * row))
     rest = jnp.zeros((send_ref.shape[1] - 2 * rhs_rows - 2, skel), F32)
     fill(send_ref, jnp.concatenate([coeff, lifted, total, along, rest], axis=0))
+    shift_ref[...] = base + times_t(row, basis)
 
 
 def half_again_kernel(
@@ -378,7 +419,7 @@
     keep = along / curve
     shift = shift_ref[...]
     rhs = rhs_ref[...]
-    row = (far + times_t(top, pair(lift_ref[0]))) * THIRD
+    row = (far + times_t(top, pair(lift_ref[0]))) * 3.0
     residual = keep * rhs - alpha * shift
     second = (base_ref[...] + near_b_ref[...]) + times_t(row, pair(basis_ref[...]))
     image = keep * (shift + SHIFT * rhs) - alpha * second
@@ -441,26 +482,21 @@
     rows = -(-(dim + 2 * rhs_rows) // 8) * 8
     rows_next = -(-(2 * rhs_rows + 2) // 8) * 8
     room = 8 + (2 * groups * half * rows * skel * 4 + 4 * half * skel * skel * 4) // MIB
-    inputs = [points, rhs, basis, transfer, inv_scale, links, leaf_skel]
+    mine_shape = (dim + 2 * rhs_rows, skel)
+    inputs = [points, rhs, basis, transfer, inv_scale, links, leaf_skel, group_skel]
     scratch = [pltpu.VMEM(value.shape, value.dtype) for value in inputs]
     for index in (4, 5):
         scratch[index] = pltpu.SMEM(inputs[index].shape, inputs[index].dtype)
-    beside, send, weight = call(
-        prepare_kernel,
-        [((dim + rhs_rows, width), F32), ((groups * half, rows, skel), F32), ((8, skel), F32)],
-        inputs, space=pltpu.HBM, scratch=scratch + [pltpu.SemaphoreType.DMA((7,))],
+    beside, send, weight, mine = call(
+        functools.partial(prepare_kernel, groups=groups),
+        [((dim + rhs_rows, width), F32), ((groups * half, rows, skel), F32), ((8, skel), F32),
+         (mine_shape, F32)],
+        inputs, space=pltpu.HBM, scratch=scratch + [pltpu.SemaphoreType.DMA((8,))],
         limit=60,
     )
     got = spread(send, members)
     beside_a = pass_on(beside, pairs_a)
     beside_b = pass_on(beside, pairs_b)
-    picks = [group_skel] + [
-        pass_on(
-            group_skel, [(i, (i + s) % groups) for i in range(groups)],
-            "grp",
-        )
-        for s in range(1, groups)
-    ]
 
     def near_part(other, vec, kind):
         return call(
@@ -468,28 +504,37 @@
             [weight, beside, other, vec], limit=16, flops=4 * 10**9,
         )[0]
 
-    near = near_part(beside, beside, 0)
+    def self_part(vec):
+        return call(
+            self_kernel, [(wide, F32)], [weight, beside, vec],
+            scratch=[pltpu.VMEM((width, width), BF16)] * 2, limit=16, flops=4 * 10**9,
+        )[0]
+
+    near = self_part(beside)
     near_a = near_part(beside_a, beside_a, 1)
     near_b = near_part(beside_b, beside_b, 2)
     peer = pass_on(got, pairs_a)
-    part, left, high, low, far, base, coeff, gram = call(
+    base, coeff, gram, mine = call(
+        base_kernel, [(wide, F32), (small, F32), ((skel, skel), F32), (mine_shape, F32)],
+        [mine, near, near_a, rhs, noise, basis], flops=10**9,
+    )
+    part, left, high, low, far = call(
         functools.partial(half_kernel, groups=groups),
         [((groups, dim + rhs_rows, skel), F32), ((skel, skel), BF16), far_shape, far_shape,
-         (small, F32), (wide, F32), (small, F32), ((skel, skel), F32)],
-        [got, *picks, send, near, near_a, rhs, noise, basis],
-        limit=room, flops=10**9,
+         (small, F32)],
+        [got, mine], limit=room, flops=10**9,
     )
     shift, send, top_high, top_low, peer_high, peer_low = call(
         functools.partial(first_image_kernel, groups=groups),
         [(wide, F32), ((groups * half, rows_next, skel), F32), top_shape, top_shape,
          far_shape, far_shape],
-        [peer, *picks, near_b, part, left, far, base, coeff, gram, rhs, transfer, basis],
+        [peer, near_b, part, left, far, base, coeff, gram, mine, rhs, transfer, basis],
         limit=room,
     )
     got = spread(send, members)
     shift_a = pass_on(shift, pairs_a)
     shift_b = pass_on(shift, pairs_b)
-    near = near_part(beside, shift, 0)
+    near = self_part(shift)
     near_a = near_part(beside_a, shift_a, 1)
     near_b = near_part(beside_b, shift_b, 2)
     peer = pass_on(got, pairs_a)

time: 61.6 us -> 60.6 us (0.984)
  Pallas kernels: 21.5 us -> 19.4 us
  waiting for transfers between devices: 12.5 us -> 14.3 us
  starting transfers between devices: 16.7 us -> 16 us
    ppermute x7 -> x6, starting transfers between devices: 5.21 us -> 2.65 us  [pass_on(): return lax.ppermute(value, axis, pairs)]
    pallas_call x12 -> x13, Pallas kernels: 21.5 us -> 19.4 us  [call(): pl.pallas_call(kernel, out_shape=[jax.ShapeDtypeStruct(s, d) for s, d in...]
    all_to_all x2, starting transfers between devices: 11.4 us -> 13.4 us  [spread(): lax.all_to_all(value, ('grp', 'leaf'), 0, 0, tiled=True, axis_index_group...]
    all_to_all x2, waiting for transfers between devices: 12.5 us -> 14.2 us  [spread(): lax.all_to_all(value, ('grp', 'leaf'), 0, 0, tiled=True, axis_index_group...]
  transfers between devices with their start and end apart: 9 -> 8, of which waited for: 2 -> 2; matrix products, arithmetic and copies ran while one was open for 0% -> 0% of each run, Pallas kernels for 25% -> 22%
where the time goes in v3:
time: 60.6 us; the launch traced here: 60.2 us
  Pallas kernels  19.4 us (32%)
  starting transfers between devices  16 us (26%)
  waiting for transfers between devices  14.3 us (24%)
  blocking collectives  9.64 us (16%)
  between operations  0.78 us (1%)
    pallas_call x13, Pallas kernels, call(): pl.pallas_call(kernel, out_shape=[jax.ShapeDtypeStruct(s, d) for s, d in...  19.4 us
    all_to_all x2, waiting for transfers between devices, spread(): lax.all_to_all(value, ('grp', 'leaf'), 0, 0, tiled=True, axis_index_group...  14.2 us
    all_to_all x2, starting transfers between devices, spread(): lax.all_to_all(value, ('grp', 'leaf'), 0, 0, tiled=True, axis_index_group...  13.4 us
    all_to_all x1, blocking collectives, spread(): lax.all_to_all(value, ('grp', 'leaf'), 0, 0, tiled=True, axis_index_group...  9.64 us
    ppermute x6, starting transfers between devices, pass_on(): return lax.ppermute(value, axis, pairs)  2.65 us
  transfers between devices with their start and end apart: 8, of which 2 were waited for; matrix products, arithmetic and copies ran while one was open for 0% of the time, Pallas kernels for 22%

profile of v3, /device:TPU:0, one launch (start us, length us, event | category | flops | bytes accessed | tf_op | source)
XLA Modules:
  0.0 60.2 jit_solution(15973200395740860142)
XLA Ops:
  0.6 2.4 %shard_map.104 = (f32[24,1024]{1,0:T(8,128)}, f32[16,40,128]{2,1,0:T(8,128)}, f32[8,128]{1,0:T(8,128)}, f32[40,128]{1,0:T(8,128)}) custom-call(f32[8,1024]{1,0:T(8,128)} %points_hbm.1, f32[16,1024]{1,0:T(8,128)} %rhs_ref.5, f32[1024,128]{1,0:T(8,128)} %basis_ref.3, f32[1,128,128]{2,1,0:T(8,128)} %lift_ref.1, f32[8]{0:T(128)} %scale_hbm.1, s32[1,2]{1,0:T(1,128)} %links_hbm.1, ...), custom_call_target="tpu_custom_call" | custom-call | flops 1000000 | bytes 1048576 | tf_op jit(solution)/shard_map/pallas_call | solution.py:140
  3.0 0.6 collective-permute-start.2
  3.6 0.7 %collective-permute-start.1 = (f32[24,1024]{1,0:T(8,128)}, f32[24,1024]{1,0:T(8,128)S(1)}, u32[]{:S(2)}, u32[]{:S(2)}) collective-permute-start(f32[24,1024]{1,0:T(8,128)} %get-tuple-element.30.own_ref.vec_ref), channel_id=1, source_target_pairs={{1,2},{2,1},{3,4},{4,3},{5,6},{6,5},{7,8},{8,7},{9,10},{10,9},{11,... | collective-permute-start | bytes 294920 | tf_op jit(solution)/shard_map/ppermute | solution.py:461
  4.2 0.0 copy-start.3
  4.2 0.0 copy-start.6
  4.2 9.9 %all-to-all-start = ((f32[16,40,128]{2,1,0:T(8,128)}), f32[16,40,128]{2,1,0:T(8,128)S(1)}, u32[]{:S(2)}, u32[]{:S(2)}) async-start(f32[16,40,128]{2,1,0:T(8,128)} %get-tuple-element.28), calls=%async_computation | async-start | bytes 655360 | tf_op jit(solution)/shard_map/all_to_all | solution.py:455
  14.1 0.0 copy-done.3
  14.1 0.0 copy-done.6
  14.1 1.8 %shard_map.106.near_ref = f32[16,1024]{1,0:T(8,128)S(1)} custom-call(f32[8,128]{1,0:T(8,128)S(1)} %copy-done.6, f32[24,1024]{1,0:T(8,128)S(1)} %copy-done.3, f32[24,1024]{1,0:T(8,128)S(1)} %copy-done.3), custom_call_target="tpu_custom_call" | custom-call | flops 4000000000 | bytes 1048576 | tf_op jit(solution)/shard_map/pallas_call | solution.py:140
  15.9 0.0 collective-permute-done.2.other_ref.vec_ref
  15.9 2.0 %shard_map.107.near_a_ref = f32[16,1024]{1,0:T(8,128)S(1)} custom-call(f32[8,128]{1,0:T(8,128)S(1)} %copy-done.6, f32[24,1024]{1,0:T(8,128)S(1)} %copy-done.3, f32[24,1024]{1,0:T(8,128)S(1)} %collective-permute-done.2.other_ref.vec_ref, f32[24,1024]{1,0:T(8,128)S(1)} %collective-permute-done.2.other_ref.vec_ref), custom_call_target="tpu_custom_call" | custom-call | flops 4000000000 | bytes 1048576 | tf_op jit(solution)/shard_map/pallas_call | solution.py:140
  17.9 0.0 copy-start
  18.0 0.0 copy-start.1
  18.0 0.0 copy-start.4
  18.0 0.0 copy-start.5
  18.0 7.7 %all-to-all-done.got_ref = f32[16,40,128]{2,1,0:T(8,128)S(1)} async-done(((f32[16,40,128]{2,1,0:T(8,128)}), f32[16,40,128]{2,1,0:T(8,128)S(1)}, u32[]{:S(2)}, u32[]{:S(2)}) %all-to-all-start) | async-done | bytes 327712 | tf_op jit(solution)/shard_map/all_to_all | solution.py:455
  25.7 0.0 collective-permute-start
  25.7 0.0 collective-permute-done.1.other_ref.vec_ref
  25.7 2.0 %shard_map.105.refs_1_ = f32[16,1024]{1,0:T(8,128)S(1)} custom-call(f32[8,128]{1,0:T(8,128)S(1)} %copy-done.6, f32[24,1024]{1,0:T(8,128)S(1)} %copy-done.3, f32[24,1024]{1,0:T(8,128)S(1)} %collective-permute-done.1.other_ref.vec_ref, f32[24,1024]{1,0:T(8,128)S(1)} %collective-permute-done.1.other_ref.vec_ref), custom_call_target="tpu_custom_call" | custom-call | flops 4000000000 | bytes 1048576 | tf_op jit(solution)/shard_map/pallas_call | solution.py:140
  27.7 0.0 copy-done
  27.7 0.0 copy-done.1
  27.7 0.0 copy-done.4
  27.7 0.0 copy-done.5
  27.7 0.4 shard_map.108
  28.1 0.0 copy-start.2
  28.2 0.8 %shard_map.109 = (f32[2,24,128]{2,1,0:T(8,128)S(1)}, bf16[128,128]{1,0:T(8,128)(2,1)S(1)}, bf16[1,128,1024]{2,1,0:T(8,128)(2,1)S(1)}, bf16[1,128,1024]{2,1,0:T(8,128)(2,1)S(1)}, f32[16,128]{1,0:T(8,128)S(1)}) custom-call(f32[16,40,128]{2,1,0:T(8,128)S(1)} %all-to-all-done.got_ref, f32[40,128]{1,0:T(8,128)S(1)} %get-tuple-element.32.mine_ref.refs_8_), custom_call_target="tpu_custom_call" | custom-call | flops 1000000000 | bytes 1048576 | tf_op jit(solution)/shard_map/pallas_call | solution.py:140
  28.9 0.0 collective-permute-done.refs_0_
  28.9 0.1 copy-done.2
  29.0 1.9 %shard_map.110 = (f32[16,1024]{1,0:T(8,128)S(1)}, f32[16,40,128]{2,1,0:T(8,128)}, bf16[128,256]{1,0:T(8,128)(2,1)S(1)}, bf16[128,256]{1,0:T(8,128)(2,1)S(1)}, bf...) custom-call(f32[16,40,128]{2,1,0:T(8,128)S(1)} %collective-permute-done.refs_0_, ...), custom_call_target="tpu_custom_call" | custom-call | flops 1000000 | bytes 1048576 | tf_op jit(solution)/shard_map/pallas_call | solution.py:140
  30.9 3.5 %all-to-all-start.1 = ((f32[16,40,128]{2,1,0:T(8,128)}), f32[16,40,128]{2,1,0:T(8,128)S(1)}, u32[]{:S(2)}, u32[]{:S(2)}) async-start(f32[16,40,128]{2,1,0:T(8,128)} %get-tuple-element.39), calls=%async_computation.1 | async-start | bytes 655360 | tf_op jit(solution)/shard_map/all_to_all | solution.py:455
  34.5 0.6 collective-permute-start.5
  35.0 1.8 %shard_map.112.near_ref = f32[16,1024]{1,0:T(8,128)S(1)} custom-call(f32[8,128]{1,0:T(8,128)S(1)} %copy-done.6, f32[24,1024]{1,0:T(8,128)S(1)} %copy-done.3, f32[16,1024]{1,0:T(8,128)S(1)} %get-tuple-element.40.vec_ref.shift_ref), custom_call_target="tpu_custom_call" | custom-call | flops 4000000000 | bytes 1048576 | tf_op jit(solution)/shard_map/pallas_call | solution.py:140
  36.8 0.9 %collective-permute-start.4 = (f32[16,1024]{1,0:T(8,128)S(1)}, f32[16,1024]{1,0:T(8,128)S(1)}, u32[]{:S(2)}, u32[]{:S(2)}) collective-permute-start(f32[16,1024]{1,0:T(8,128)S(1)} %get-tuple-element.40.vec_ref.shift_ref), channel_id=1, source_target_pairs={{1,2},{2,1},{3,4},{4,3},{5,6},{6,5},{7,8},{8,7},{9,10},{10,9},{11,... | collective-permute-start | bytes 196616 | tf_op jit(solution)/shard_map/ppermute | solution.py:461
  37.7 0.0 collective-permute-done.5.vec_ref
  37.7 2.0 %shard_map.113.near_a_ref = f32[16,1024]{1,0:T(8,128)S(1)} custom-call(f32[8,128]{1,0:T(8,128)S(1)} %copy-done.6, f32[24,1024]{1,0:T(8,128)S(1)} %copy-done.3, f32[24,1024]{1,0:T(8,128)S(1)} %collective-permute-done.2.other_ref.vec_ref, f32[16,1024]{1,0:T(8,128)S(1)} %collective-permute-done.5.vec_ref), custom_call_target="tpu_custom_call" | custom-call | flops 4000000000 | bytes 1048576 | tf_op jit(solution)/shard_map/pallas_call | solution.py:140
  39.7 6.6 %all-to-all-done.1.got_ref = f32[16,40,128]{2,1,0:T(8,128)S(1)} async-done(((f32[16,40,128]{2,1,0:T(8,128)}), f32[16,40,128]{2,1,0:T(8,128)S(1)}, u32[]{:S(2)}, u32[]{:S(2)}) %all-to-all-start.1) | async-done | bytes 327712 | tf_op jit(solution)/shard_map/all_to_all | solution.py:455
  46.3 0.0 collective-permute-start.3
  46.3 0.0 collective-permute-done.4.vec_ref
  46.3 2.0 %shard_map.111.near_b_ref = f32[16,1024]{1,0:T(8,128)S(1)} custom-call(f32[8,128]{1,0:T(8,128)S(1)} %copy-done.6, f32[24,1024]{1,0:T(8,128)S(1)} %copy-done.3, f32[24,1024]{1,0:T(8,128)S(1)} %collective-permute-done.1.other_ref.vec_ref, f32[16,1024]{1,0:T(8,128)S(1)} %collective-permute-done.4.vec_ref), custom_call_target="tpu_custom_call" | custom-call | flops 4000000000 | bytes 1048576 | tf_op jit(solution)/shard_map/pallas_call | solution.py:140
  48.3 0.3 shard_map.114
  48.6 0.0 collective-permute-done.3.got_ref
  48.6 1.1 %shard_map.115 = (f32[16,1024]{1,0:T(8,128)S(1)}, f32[16,1024]{1,0:T(8,128)S(1)}, f32[16,128]{1,0:T(8,128)S(1)}, f32[32,1,128]{2,1,0:T(1,128)S(1)}) custom-call(f32[16,40,128]{2,1,0:T(8,128)S(1)} %collective-permute-done.3.got_ref, f32[16,1024]{1,0:T(8,128)S(1)} %shard_map.111.near_b_ref, f32[2,24,128]{2,1,0:T(8,128)S(1)} %get-tuple-element.43.part_ref, ...), custom_call_target="tpu_custom_call" | custom-call | flops 1000000 | bytes 1048576 | tf_op jit(solution)/shard_map/pallas_call | solution.py:140
  49.7 9.6 %all_to_all.15.got_ref = f32[32,1,128]{2,1,0:T(1,128)S(1)} all-to-all(f32[32,1,128]{2,1,0:T(1,128)S(1)} %get-tuple-element.50), channel_id=1, replica_groups=mesh['grp'=2,'leaf'=16] {'grp','leaf'}, dimensions={0} | all-to-all | bytes 32768 | tf_op jit(solution)/shard_map/all_to_all | solution.py:455
  59.4 0.9 %shard_map.116 = (f32[16,1024]{1,0:T(8,128)}, f32[16,1024]{1,0:T(8,128)}) custom-call(f32[32,1,128]{2,1,0:T(1,128)S(1)} %all_to_all.15.got_ref, f32[16,128]{1,0:T(8,128)S(1)} %get-tuple-element.51.alpha_ref, f32[16,1024]{1,0:T(8,128)S(1)} %copy-done.1, f32[16,1024]{1,0:T(8,128)S(1)} %get-tuple-element.40.vec_ref.shift_ref, ...), custom_call_target="tpu_custom_call" | custom-call | flops 1000000 | bytes 1048576 | tf_op jit(solution)/shard_map/pallas_call | solution.py:140
Async XLA Ops:
  3.0 12.9 %collective-permute-start.2 = (f32[24,1024]{1,0:T(8,128)}, f32[24,1024]{1,0:T(8,128)S(1)}, u32[]{:S(2)}, u32[]{:S(2)}) collective-permute-start(f32[24,1024]{1,0:T(8,128)} %get-tuple-element.30.own_ref.vec_ref), channel_id=1, source_target_pairs={{0,1},{1,0},{2,3},{3,2},{4,5},{5,4},{6,7},{7,6},{8,9},{9,8},{10,11... | collective-permute-start | bytes 294920 | tf_op jit(solution)/shard_map/ppermute | solution.py:461
  3.6 22.1 %collective-permute-start.1 = (f32[24,1024]{1,0:T(8,128)}, f32[24,1024]{1,0:T(8,128)S(1)}, u32[]{:S(2)}, u32[]{:S(2)}) collective-permute-start(f32[24,1024]{1,0:T(8,128)} %get-tuple-element.30.own_ref.vec_ref), channel_id=1, source_target_pairs={{1,2},{2,1},{3,4},{4,3},{5,6},{6,5},{7,8},{8,7},{9,10},{10,9},{11,... | collective-permute-start | bytes 294920 | tf_op jit(solution)/shard_map/ppermute | solution.py:461
  4.2 9.9 %copy-start.3 = (f32[24,1024]{1,0:T(8,128)S(1)}, f32[24,1024]{1,0:T(8,128)}, u32[]{:S(2)}) copy-start(f32[24,1024]{1,0:T(8,128)} %get-tuple-element.30.own_ref.vec_ref) | copy-start | bytes 294916
  4.2 9.9 %copy-start.6 = (f32[8,128]{1,0:T(8,128)S(1)}, f32[8,128]{1,0:T(8,128)}, u32[]{:S(2)}) copy-start(f32[8,128]{1,0:T(8,128)} %get-tuple-element.29.weight_ref) | copy-start | bytes 12292
  4.2 21.4 %all-to-all-start = ((f32[16,40,128]{2,1,0:T(8,128)}), f32[16,40,128]{2,1,0:T(8,128)S(1)}, u32[]{:S(2)}, u32[]{:S(2)}) async-start(f32[16,40,128]{2,1,0:T(8,128)} %get-tuple-element.28), calls=%async_computation | async-start | bytes 655360 | tf_op jit(solution)/shard_map/all_to_all | solution.py:455
  17.9 9.7 %copy-start = (f32[1024,128]{1,0:T(8,128)S(1)}, f32[1024,128]{1,0:T(8,128)}, u32[]{:S(2)}) copy-start(f32[1024,128]{1,0:T(8,128)} %basis_ref.3) | copy-start | bytes 1572868
  18.0 9.7 %copy-start.1 = (f32[16,1024]{1,0:T(8,128)S(1)}, f32[16,1024]{1,0:T(8,128)}, u32[]{:S(2)}) copy-start(f32[16,1024]{1,0:T(8,128)} %rhs_ref.5) | copy-start | bytes 196612
  18.0 9.8 %copy-start.4 = (f32[40,128]{1,0:T(8,128)S(1)}, f32[40,128]{1,0:T(8,128)}, u32[]{:S(2)}) copy-start(f32[40,128]{1,0:T(8,128)} %get-tuple-element.31.mine_ref) | copy-start | bytes 61444
  18.0 9.7 %copy-start.5 = (f32[1024]{0:T(1024)S(1)}, f32[1024]{0:T(1024)}, u32[]{:S(2)}) copy-start(f32[1024]{0:T(1024)} %param.13) | copy-start | bytes 12292
  25.7 3.2 %collective-permute-start = (f32[16,40,128]{2,1,0:T(8,128)S(1)}, f32[16,40,128]{2,1,0:T(8,128)S(1)}, u32[]{:S(2)}, u32[]{:S(2)}) collective-permute-start(f32[16,40,128]{2,1,0:T(8,128)S(1)} %all-to-all-done.got_ref), channel_id=1, source_target_pairs={{0,1},{1,0},{2,3},{3,2},{4,5},{5,4},{6,7},{7,6},{8,9},{9,8},{10,11... | collective-permute-start | bytes 983048 | tf_op jit(solution)/shard_map/ppermute | solution.py:461
  28.1 0.8 %copy-start.2 = (f32[1,128,128]{2,1,0:T(8,128)S(1)}, f32[1,128,128]{2,1,0:T(8,128)}, u32[]{:S(2)}) copy-start(f32[1,128,128]{2,1,0:T(8,128)} %lift_ref.1) | copy-start | bytes 196612
  30.9 15.4 %all-to-all-start.1 = ((f32[16,40,128]{2,1,0:T(8,128)}), f32[16,40,128]{2,1,0:T(8,128)S(1)}, u32[]{:S(2)}, u32[]{:S(2)}) async-start(f32[16,40,128]{2,1,0:T(8,128)} %get-tuple-element.39), calls=%async_computation.1 | async-start | bytes 655360 | tf_op jit(solution)/shard_map/all_to_all | solution.py:455
  34.5 3.2 %collective-permute-start.5 = (f32[16,1024]{1,0:T(8,128)S(1)}, f32[16,1024]{1,0:T(8,128)S(1)}, u32[]{:S(2)}, u32[]{:S(2)}) collective-permute-start(f32[16,1024]{1,0:T(8,128)S(1)} %get-tuple-element.40.vec_ref.shift_ref), channel_id=1, source_target_pairs={{0,1},{1,0},{2,3},{3,2},{4,5},{5,4},{6,7},{7,6},{8,9},{9,8},{10,11... | collective-permute-start | bytes 196616 | tf_op jit(solution)/shard_map/ppermute | solution.py:461
  36.8 9.5 %collective-permute-start.4 = (f32[16,1024]{1,0:T(8,128)S(1)}, f32[16,1024]{1,0:T(8,128)S(1)}, u32[]{:S(2)}, u32[]{:S(2)}) collective-permute-start(f32[16,1024]{1,0:T(8,128)S(1)} %get-tuple-element.40.vec_ref.shift_ref), channel_id=1, source_target_pairs={{1,2},{2,1},{3,4},{4,3},{5,6},{6,5},{7,8},{8,7},{9,10},{10,9},{11,... | collective-permute-start | bytes 196616 | tf_op jit(solution)/shard_map/ppermute | solution.py:461
  46.3 2.3 %collective-permute-start.3 = (f32[16,40,128]{2,1,0:T(8,128)S(1)}, f32[16,40,128]{2,1,0:T(8,128)S(1)}, u32[]{:S(2)}, u32[]{:S(2)}) collective-permute-start(f32[16,40,128]{2,1,0:T(8,128)S(1)} %all-to-all-done.1.got_ref), channel_id=1, source_target_pairs={{0,1},{1,0},{2,3},{3,2},{4,5},{5,4},{6,7},{7,6},{8,9},{9,8},{10,11... | collective-permute-start | bytes 983048 | tf_op jit(solution)/shard_map/ppermute | solution.py:461

commit v4 on v3

--- a/solution.py
+++ b/solution.py
@@ -400,9 +400,15 @@
     base_ref[...] = noise_ref[...] * shift_ref[...] + (near_ref[...] + near_a_ref[...])
 
 
+def lift_kernel(lift_ref, high_ref, low_ref, out_high_ref, out_low_ref):
+    parts = triple(lift_ref[0])
+    both = fold(raw(parts, high_ref[...]) + raw(parts, low_ref[...]))
+    out_high_ref[...], out_low_ref[...] = split2(both)
+
+
 def second_image_kernel(
     got_ref, near_b_ref, part_ref, far_ref, base_ref, high_ref, low_ref, top_high_ref, top_low_ref,
-    rhs_ref, shift_ref, lift_ref, basis_ref, residual_ref, image_ref, alpha_ref, send_ref,
+    rhs_ref, shift_ref, basis_ref, residual_ref, image_ref, alpha_ref, send_ref,
 ):
     rhs_rows, skel = far_ref.shape
     groups = part_ref.shape[0]
@@ -419,7 +425,7 @@
     keep = along / curve
     shift = shift_ref[...]
     rhs = rhs_ref[...]
-    row = (far + times_t(top, pair(lift_ref[0]))) * 3.0
+    row = (far + top) * 3.0
     residual = keep * rhs - alpha * shift
     second = (base_ref[...] + near_b_ref[...]) + times_t(row, pair(basis_ref[...]))
     image = keep * (shift + SHIFT * rhs) - alpha * second
@@ -538,6 +544,9 @@
     near_a = near_part(beside_a, shift_a, 1)
     near_b = near_part(beside_b, shift_b, 2)
     peer = pass_on(got, pairs_a)
+    top_high, top_low = call(
+        lift_kernel, [top_shape, top_shape], [transfer, top_high, top_low], flops=10**8,
+    )
     part, far, base = call(
         half_again_kernel,
         [((groups, rows_next - rhs_rows, skel), F32), (small, F32), (wide, F32)],
@@ -548,7 +557,7 @@
         second_image_kernel,
         [(wide, F32), (wide, F32), (small, F32), ((boxes * groups, 1, skel), F32)],
         [peer, near_b, part, far, base, peer_high, peer_low, top_high, top_low,
-         rhs, shift, transfer, basis],
+         rhs, shift, basis],
         limit=room,
     )
     got = spread(send)

time: 60.6 us -> 60.6 us (level)
    pallas_call x13 -> x14, Pallas kernels: 19.4 us -> 19.6 us  [call(): pl.pallas_call(kernel, out_shape=[jax.ShapeDtypeStruct(s, d) for s, d in...]
where the time goes in v4:
time: 60.6 us; the launch traced here: 60.2 us
  Pallas kernels  19.6 us (32%)
  starting transfers between devices  16 us (26%)
  waiting for transfers between devices  14 us (23%)
  blocking collectives  9.64 us (16%)
  between operations  0.79 us (1%)
    pallas_call x14, Pallas kernels, call(): pl.pallas_call(kernel, out_shape=[jax.ShapeDtypeStruct(s, d) for s, d in...  19.6 us
    all_to_all x2, waiting for transfers between devices, spread(): lax.all_to_all(value, ('grp', 'leaf'), 0, 0, tiled=True, axis_index_group...  14 us
    all_to_all x2, starting transfers between devices, spread(): lax.all_to_all(value, ('grp', 'leaf'), 0, 0, tiled=True, axis_index_group...  13.4 us
    all_to_all x1, blocking collectives, spread(): lax.all_to_all(value, ('grp', 'leaf'), 0, 0, tiled=True, axis_index_group...  9.64 us
    ppermute x6, starting transfers between devices, pass_on(): return lax.ppermute(value, axis, pairs)  2.65 us
  transfers between devices with their start and end apart: 8, of which 2 were waited for; matrix products, arithmetic and copies ran while one was open for 0% of the time, Pallas kernels for 22%

profile of v4, /device:TPU:0, one launch (start us, length us, event | category | flops | bytes accessed | tf_op | source)
XLA Modules:
  0.0 60.2 jit_solution(13468387475194492033)
XLA Ops:
  0.6 2.3 %shard_map.104 = (f32[24,1024]{1,0:T(8,128)}, f32[16,40,128]{2,1,0:T(8,128)}, f32[8,128]{1,0:T(8,128)}, f32[40,128]{1,0:T(8,128)}) custom-call(f32[8,1024]{1,0:T(8,128)} %points_hbm.1, f32[16,1024]{1,0:T(8,128)} %rhs_ref.5, f32[1024,128]{1,0:T(8,128)} %basis_ref.3, f32[1,128,128]{2,1,0:T(8,128)} %lift_ref.1, f32[8]{0:T(128)} %scale_hbm.1, s32[1,2]{1,0:T(1,128)} %links_hbm.1, ...), custom_call_target="tpu_custom_call" | custom-call | flops 1000000 | bytes 1048576 | tf_op jit(solution)/shard_map/pallas_call | solution.py:140
  3.0 0.6 collective-permute-start.2
  3.5 0.7 %collective-permute-start.1 = (f32[24,1024]{1,0:T(8,128)}, f32[24,1024]{1,0:T(8,128)S(1)}, u32[]{:S(2)}, u32[]{:S(2)}) collective-permute-start(f32[24,1024]{1,0:T(8,128)} %get-tuple-element.32.own_ref.vec_ref), channel_id=1, source_target_pairs={{1,2},{2,1},{3,4},{4,3},{5,6},{6,5},{7,8},{8,7},{9,10},{10,9},{11,... | collective-permute-start | bytes 294920 | tf_op jit(solution)/shard_map/ppermute | solution.py:467
  4.2 0.0 copy-start.3
  4.2 0.0 copy-start.6
  4.2 9.9 %all-to-all-start = ((f32[16,40,128]{2,1,0:T(8,128)}), f32[16,40,128]{2,1,0:T(8,128)S(1)}, u32[]{:S(2)}, u32[]{:S(2)}) async-start(f32[16,40,128]{2,1,0:T(8,128)} %get-tuple-element.30), calls=%async_computation | async-start | bytes 655360 | tf_op jit(solution)/shard_map/all_to_all | solution.py:461
  14.1 0.0 copy-done.3
  14.1 0.0 copy-done.6
  14.1 1.8 %shard_map.106.near_ref = f32[16,1024]{1,0:T(8,128)S(1)} custom-call(f32[8,128]{1,0:T(8,128)S(1)} %copy-done.6, f32[24,1024]{1,0:T(8,128)S(1)} %copy-done.3, f32[24,1024]{1,0:T(8,128)S(1)} %copy-done.3), custom_call_target="tpu_custom_call" | custom-call | flops 4000000000 | bytes 1048576 | tf_op jit(solution)/shard_map/pallas_call | solution.py:140
  15.9 0.0 collective-permute-done.2.other_ref.vec_ref
  15.9 2.0 %shard_map.107.near_a_ref = f32[16,1024]{1,0:T(8,128)S(1)} custom-call(f32[8,128]{1,0:T(8,128)S(1)} %copy-done.6, f32[24,1024]{1,0:T(8,128)S(1)} %copy-done.3, f32[24,1024]{1,0:T(8,128)S(1)} %collective-permute-done.2.other_ref.vec_ref, f32[24,1024]{1,0:T(8,128)S(1)} %collective-permute-done.2.other_ref.vec_ref), custom_call_target="tpu_custom_call" | custom-call | flops 4000000000 | bytes 1048576 | tf_op jit(solution)/shard_map/pallas_call | solution.py:140
  17.9 0.0 copy-start
  17.9 0.0 copy-start.1
  17.9 0.0 copy-start.4
  18.0 0.0 copy-start.5
  18.0 7.7 %all-to-all-done.got_ref = f32[16,40,128]{2,1,0:T(8,128)S(1)} async-done(((f32[16,40,128]{2,1,0:T(8,128)}), f32[16,40,128]{2,1,0:T(8,128)S(1)}, u32[]{:S(2)}, u32[]{:S(2)}) %all-to-all-start) | async-done | bytes 327712 | tf_op jit(solution)/shard_map/all_to_all | solution.py:461
  25.7 0.0 collective-permute-start
  25.7 0.0 collective-permute-done.1.other_ref.vec_ref
  25.7 2.0 %shard_map.105.refs_1_ = f32[16,1024]{1,0:T(8,128)S(1)} custom-call(f32[8,128]{1,0:T(8,128)S(1)} %copy-done.6, f32[24,1024]{1,0:T(8,128)S(1)} %copy-done.3, f32[24,1024]{1,0:T(8,128)S(1)} %collective-permute-done.1.other_ref.vec_ref, f32[24,1024]{1,0:T(8,128)S(1)} %collective-permute-done.1.other_ref.vec_ref), custom_call_target="tpu_custom_call" | custom-call | flops 4000000000 | bytes 1048576 | tf_op jit(solution)/shard_map/pallas_call | solution.py:140
  27.7 0.0 copy-done
  27.7 0.0 copy-done.1
  27.7 0.0 copy-done.4
  27.7 0.0 copy-done.5
  27.7 0.4 shard_map.108
  28.1 0.0 copy-start.2
  28.1 0.8 %shard_map.109 = (f32[2,24,128]{2,1,0:T(8,128)S(1)}, bf16[128,128]{1,0:T(8,128)(2,1)S(1)}, bf16[1,128,1024]{2,1,0:T(8,128)(2,1)S(1)}, bf16[1,128,1024]{2,1,0:T(8,128)(2,1)S(1)}, f32[16,128]{1,0:T(8,128)S(1)}) custom-call(f32[16,40,128]{2,1,0:T(8,128)S(1)} %all-to-all-done.got_ref, f32[40,128]{1,0:T(8,128)S(1)} %get-tuple-element.34.mine_ref.refs_8_), custom_call_target="tpu_custom_call" | custom-call | flops 1000000000 | bytes 1048576 | tf_op jit(solution)/shard_map/pallas_call | solution.py:140
  28.9 0.0 collective-permute-done.refs_0_
  28.9 0.1 copy-done.2
  29.0 1.9 %shard_map.110 = (f32[16,1024]{1,0:T(8,128)S(1)}, f32[16,40,128]{2,1,0:T(8,128)}, bf16[128,256]{1,0:T(8,128)(2,1)S(1)}, bf16[128,256]{1,0:T(8,128)(2,1)S(1)}, bf...) custom-call(f32[16,40,128]{2,1,0:T(8,128)S(1)} %collective-permute-done.refs_0_, ...), custom_call_target="tpu_custom_call" | custom-call | flops 1000000 | bytes 1048576 | tf_op jit(solution)/shard_map/pallas_call | solution.py:140
  30.9 3.5 %all-to-all-start.1 = ((f32[16,40,128]{2,1,0:T(8,128)}), f32[16,40,128]{2,1,0:T(8,128)S(1)}, u32[]{:S(2)}, u32[]{:S(2)}) async-start(f32[16,40,128]{2,1,0:T(8,128)} %get-tuple-element.41), calls=%async_computation.1 | async-start | bytes 655360 | tf_op jit(solution)/shard_map/all_to_all | solution.py:461
  34.5 0.6 collective-permute-start.5
  35.0 1.8 %shard_map.112.near_ref = f32[16,1024]{1,0:T(8,128)S(1)} custom-call(f32[8,128]{1,0:T(8,128)S(1)} %copy-done.6, f32[24,1024]{1,0:T(8,128)S(1)} %copy-done.3, f32[16,1024]{1,0:T(8,128)S(1)} %get-tuple-element.42.vec_ref.shift_ref), custom_call_target="tpu_custom_call" | custom-call | flops 4000000000 | bytes 1048576 | tf_op jit(solution)/shard_map/pallas_call | solution.py:140
  36.8 0.9 %collective-permute-start.4 = (f32[16,1024]{1,0:T(8,128)S(1)}, f32[16,1024]{1,0:T(8,128)S(1)}, u32[]{:S(2)}, u32[]{:S(2)}) collective-permute-start(f32[16,1024]{1,0:T(8,128)S(1)} %get-tuple-element.42.vec_ref.shift_ref), channel_id=1, source_target_pairs={{1,2},{2,1},{3,4},{4,3},{5,6},{6,5},{7,8},{8,7},{9,10},{10,9},{11,... | collective-permute-start | bytes 196616 | tf_op jit(solution)/shard_map/ppermute | solution.py:467
  37.7 0.3 shard_map.115
  37.9 0.0 collective-permute-done.5.vec_ref
  38.0 2.0 %shard_map.113.near_a_ref = f32[16,1024]{1,0:T(8,128)S(1)} custom-call(f32[8,128]{1,0:T(8,128)S(1)} %copy-done.6, f32[24,1024]{1,0:T(8,128)S(1)} %copy-done.3, f32[24,1024]{1,0:T(8,128)S(1)} %collective-permute-done.2.other_ref.vec_ref, f32[16,1024]{1,0:T(8,128)S(1)} %collective-permute-done.5.vec_ref), custom_call_target="tpu_custom_call" | custom-call | flops 4000000000 | bytes 1048576 | tf_op jit(solution)/shard_map/pallas_call | solution.py:140
  40.0 6.3 %all-to-all-done.1.got_ref = f32[16,40,128]{2,1,0:T(8,128)S(1)} async-done(((f32[16,40,128]{2,1,0:T(8,128)}), f32[16,40,128]{2,1,0:T(8,128)S(1)}, u32[]{:S(2)}, u32[]{:S(2)}) %all-to-all-start.1) | async-done | bytes 327712 | tf_op jit(solution)/shard_map/all_to_all | solution.py:461
  46.3 0.0 collective-permute-start.3
  46.3 0.0 collective-permute-done.4.vec_ref
  46.3 2.0 %shard_map.111.near_b_ref = f32[16,1024]{1,0:T(8,128)S(1)} custom-call(f32[8,128]{1,0:T(8,128)S(1)} %copy-done.6, f32[24,1024]{1,0:T(8,128)S(1)} %copy-done.3, f32[24,1024]{1,0:T(8,128)S(1)} %collective-permute-done.1.other_ref.vec_ref, f32[16,1024]{1,0:T(8,128)S(1)} %collective-permute-done.4.vec_ref), custom_call_target="tpu_custom_call" | custom-call | flops 4000000000 | bytes 1048576 | tf_op jit(solution)/shard_map/pallas_call | solution.py:140
  48.3 0.3 shard_map.114
  48.6 0.0 collective-permute-done.3.got_ref
  48.6 1.1 %shard_map.116 = (f32[16,1024]{1,0:T(8,128)S(1)}, f32[16,1024]{1,0:T(8,128)S(1)}, f32[16,128]{1,0:T(8,128)S(1)}, f32[32,1,128]{2,1,0:T(1,128)S(1)}) custom-call(f32[16,40,128]{2,1,0:T(8,128)S(1)} %collective-permute-done.3.got_ref, f32[16,1024]{1,0:T(8,128)S(1)} %shard_map.111.near_b_ref, f32[2,24,128]{2,1,0:T(8,128)S(1)} %get-tuple-element.45.part_ref, ...), custom_call_target="tpu_custom_call" | custom-call | flops 1000000 | bytes 1048576 | tf_op jit(solution)/shard_map/pallas_call | solution.py:140
  49.7 9.6 %all_to_all.15.got_ref = f32[32,1,128]{2,1,0:T(1,128)S(1)} all-to-all(f32[32,1,128]{2,1,0:T(1,128)S(1)} %get-tuple-element.54), channel_id=1, replica_groups=mesh['grp'=2,'leaf'=16] {'grp','leaf'}, dimensions={0} | all-to-all | bytes 32768 | tf_op jit(solution)/shard_map/all_to_all | solution.py:461
  59.3 0.9 %shard_map.117 = (f32[16,1024]{1,0:T(8,128)}, f32[16,1024]{1,0:T(8,128)}) custom-call(f32[32,1,128]{2,1,0:T(1,128)S(1)} %all_to_all.15.got_ref, f32[16,128]{1,0:T(8,128)S(1)} %get-tuple-element.55.alpha_ref, f32[16,1024]{1,0:T(8,128)S(1)} %copy-done.1, f32[16,1024]{1,0:T(8,128)S(1)} %get-tuple-element.42.vec_ref.shift_ref, ...), custom_call_target="tpu_custom_call" | custom-call | flops 1000000 | bytes 1048576 | tf_op jit(solution)/shard_map/pallas_call | solution.py:140
Async XLA Ops:
  3.0 12.9 %collective-permute-start.2 = (f32[24,1024]{1,0:T(8,128)}, f32[24,1024]{1,0:T(8,128)S(1)}, u32[]{:S(2)}, u32[]{:S(2)}) collective-permute-start(f32[24,1024]{1,0:T(8,128)} %get-tuple-element.32.own_ref.vec_ref), channel_id=1, source_target_pairs={{0,1},{1,0},{2,3},{3,2},{4,5},{5,4},{6,7},{7,6},{8,9},{9,8},{10,11... | collective-permute-start | bytes 294920 | tf_op jit(solution)/shard_map/ppermute | solution.py:467
  3.5 22.1 %collective-permute-start.1 = (f32[24,1024]{1,0:T(8,128)}, f32[24,1024]{1,0:T(8,128)S(1)}, u32[]{:S(2)}, u32[]{:S(2)}) collective-permute-start(f32[24,1024]{1,0:T(8,128)} %get-tuple-element.32.own_ref.vec_ref), channel_id=1, source_target_pairs={{1,2},{2,1},{3,4},{4,3},{5,6},{6,5},{7,8},{8,7},{9,10},{10,9},{11,... | collective-permute-start | bytes 294920 | tf_op jit(solution)/shard_map/ppermute | solution.py:467
  4.2 9.9 %copy-start.3 = (f32[24,1024]{1,0:T(8,128)S(1)}, f32[24,1024]{1,0:T(8,128)}, u32[]{:S(2)}) copy-start(f32[24,1024]{1,0:T(8,128)} %get-tuple-element.32.own_ref.vec_ref) | copy-start | bytes 294916
  4.2 9.9 %copy-start.6 = (f32[8,128]{1,0:T(8,128)S(1)}, f32[8,128]{1,0:T(8,128)}, u32[]{:S(2)}) copy-start(f32[8,128]{1,0:T(8,128)} %get-tuple-element.31.weight_ref) | copy-start | bytes 12292
  4.2 21.4 %all-to-all-start = ((f32[16,40,128]{2,1,0:T(8,128)}), f32[16,40,128]{2,1,0:T(8,128)S(1)}, u32[]{:S(2)}, u32[]{:S(2)}) async-start(f32[16,40,128]{2,1,0:T(8,128)} %get-tuple-element.30), calls=%async_computation | async-start | bytes 655360 | tf_op jit(solution)/shard_map/all_to_all | solution.py:461
  17.9 9.7 %copy-start = (f32[1024,128]{1,0:T(8,128)S(1)}, f32[1024,128]{1,0:T(8,128)}, u32[]{:S(2)}) copy-start(f32[1024,128]{1,0:T(8,128)} %basis_ref.3) | copy-start | bytes 1572868
  17.9 9.7 %copy-start.1 = (f32[16,1024]{1,0:T(8,128)S(1)}, f32[16,1024]{1,0:T(8,128)}, u32[]{:S(2)}) copy-start(f32[16,1024]{1,0:T(8,128)} %rhs_ref.5) | copy-start | bytes 196612
  17.9 9.8 %copy-start.4 = (f32[40,128]{1,0:T(8,128)S(1)}, f32[40,128]{1,0:T(8,128)}, u32[]{:S(2)}) copy-start(f32[40,128]{1,0:T(8,128)} %get-tuple-element.33.mine_ref) | copy-start | bytes 61444
  18.0 9.7 %copy-start.5 = (f32[1024]{0:T(1024)S(1)}, f32[1024]{0:T(1024)}, u32[]{:S(2)}) copy-start(f32[1024]{0:T(1024)} %param.13) | copy-start | bytes 12292
  25.7 3.2 %collective-permute-start = (f32[16,40,128]{2,1,0:T(8,128)S(1)}, f32[16,40,128]{2,1,0:T(8,128)S(1)}, u32[]{:S(2)}, u32[]{:S(2)}) collective-permute-start(f32[16,40,128]{2,1,0:T(8,128)S(1)} %all-to-all-done.got_ref), channel_id=1, source_target_pairs={{0,1},{1,0},{2,3},{3,2},{4,5},{5,4},{6,7},{7,6},{8,9},{9,8},{10,11... | collective-permute-start | bytes 983048 | tf_op jit(solution)/shard_map/ppermute | solution.py:467
  28.1 0.8 %copy-start.2 = (f32[1,128,128]{2,1,0:T(8,128)S(1)}, f32[1,128,128]{2,1,0:T(8,128)}, u32[]{:S(2)}) copy-start(f32[1,128,128]{2,1,0:T(8,128)} %lift_ref.1) | copy-start | bytes 196612
  30.9 15.4 %all-to-all-start.1 = ((f32[16,40,128]{2,1,0:T(8,128)}), f32[16,40,128]{2,1,0:T(8,128)S(1)}, u32[]{:S(2)}, u32[]{:S(2)}) async-start(f32[16,40,128]{2,1,0:T(8,128)} %get-tuple-element.41), calls=%async_computation.1 | async-start | bytes 655360 | tf_op jit(solution)/shard_map/all_to_all | solution.py:461
  34.5 3.5 %collective-permute-start.5 = (f32[16,1024]{1,0:T(8,128)S(1)}, f32[16,1024]{1,0:T(8,128)S(1)}, u32[]{:S(2)}, u32[]{:S(2)}) collective-permute-start(f32[16,1024]{1,0:T(8,128)S(1)} %get-tuple-element.42.vec_ref.shift_ref), channel_id=1, source_target_pairs={{0,1},{1,0},{2,3},{3,2},{4,5},{5,4},{6,7},{7,6},{8,9},{9,8},{10,11... | collective-permute-start | bytes 196616 | tf_op jit(solution)/shard_map/ppermute | solution.py:467
  36.8 9.5 %collective-permute-start.4 = (f32[16,1024]{1,0:T(8,128)S(1)}, f32[16,1024]{1,0:T(8,128)S(1)}, u32[]{:S(2)}, u32[]{:S(2)}) collective-permute-start(f32[16,1024]{1,0:T(8,128)S(1)} %get-tuple-element.42.vec_ref.shift_ref), channel_id=1, source_target_pairs={{1,2},{2,1},{3,4},{4,3},{5,6},{6,5},{7,8},{8,7},{9,10},{10,9},{11,... | collective-permute-start | bytes 196616 | tf_op jit(solution)/shard_map/ppermute | solution.py:467
  46.3 2.3 %collective-permute-start.3 = (f32[16,40,128]{2,1,0:T(8,128)S(1)}, f32[16,40,128]{2,1,0:T(8,128)S(1)}, u32[]{:S(2)}, u32[]{:S(2)}) collective-permute-start(f32[16,40,128]{2,1,0:T(8,128)S(1)} %all-to-all-done.1.got_ref), channel_id=1, source_target_pairs={{0,1},{1,0},{2,3},{3,2},{4,5},{5,4},{6,7},{7,6},{8,9},{9,8},{10,11... | collective-permute-start | bytes 983048 | tf_op jit(solution)/shard_map/ppermute | solution.py:467
